TPU v7x, 32 devices: a whole 2x2x4 slice. The times are simulated.
32 devices in a mesh: gx: 32 (over z, y, x, core).
Axes of the slice: x: 2, y: 2, z: 4, core: 2. Of those that a mesh axis runs over, the one named last changes fastest.
Arguments:
- fine: bfloat16 [64, 8192, 128], P(None, 'gx'), may hold values from -6 to 6
- pattern: int32 [8, 8192], P(None, 'gx'), may hold values from 0 to 3
- stencil: bfloat16 [3, 128, 128], replicated, may hold values from -0.3125 to 0.3125
- restrict: bfloat16 [8, 4, 128, 128], replicated, may hold values from -0.5 to 0.5
- coarse_inv: bfloat16 [8, 128, 128], replicated, may hold values from -0.5 to 0.5
Outputs:
- smoothed: float32 [64, 8192, 128], P(None, 'gx')
All inputs are finite; a program needn't handle non-finite values.
Results may differ from a plain program's by a relative error of at most 0.0046.
Values may be sent and summed in bfloat16 or wider, within the bound.
No kernel may reach another device: no remote copies, remote signals or barrier semaphores. Data moves between devices by JAX's collectives and lax.ppermute only.
A program may use at most 128 MiB of HBM per device.

v0:
```python
import jax
import jax.numpy as jnp
from jax import lax
from jax.sharding import PartitionSpec as P


def padded_2(cells, sides, width):
    for axis, dim in sides:
        count = lax.axis_size(axis)
        head = lax.slice_in_dim(cells, 0, width, axis=dim)
        tail = lax.slice_in_dim(cells, cells.shape[dim] - width, cells.shape[dim], axis=dim)
        cells = jnp.concatenate(
            [
                lax.ppermute(tail, axis, [(i, (i + 1) % count) for i in range(count)]),
                cells,
                lax.ppermute(head, axis, [((i + 1) % count, i) for i in range(count)]),
            ],
            axis=dim,
        )
    return cells


def partner_2(x, axis, apart):
    return lax.ppermute(x, axis, [(i, i ^ 1 << apart) for i in range(lax.axis_size(axis))])


def shards(fine, pattern, stencil, restrict, coarse_inv):
    devices = lax.axis_size("gx")
    vectors, blocks, width = fine.shape
    levels = restrict.shape[0]
    kind_count = restrict.shape[1]
    all_blocks = blocks * devices
    padded = padded_2(fine, (("gx", 1),), 1)
    result = jnp.einsum(
        "vic,cd->vid", padded[:, :-2], stencil[0], preferred_element_type=jnp.float32
    )
    result = result + jnp.einsum(
        "vic,cd->vid", padded[:, 1:-1], stencil[1], preferred_element_type=jnp.float32
    )
    result = result + jnp.einsum(
        "vic,cd->vid", padded[:, 2:], stencil[2], preferred_element_type=jnp.float32
    )
    kinds_row = jnp.arange(kind_count, dtype=jnp.int32)
    summed = []
    kind_maps = []
    groups = []
    counts_list = []
    for level_num in range(levels):
        coarse_num = max(all_blocks // 4 ** (level_num + 1), 1)
        span_blocks = all_blocks // coarse_num
        local_span = min(span_blocks, blocks)
        local_num = blocks // local_span
        selector = pattern[level_num][:, None] == kinds_row[None, :]
        onehot = selector.astype(jnp.bfloat16).reshape(local_num, local_span, kind_count)
        grouped = jnp.einsum(
            "vjsc,jsk->vjkc",
            fine.reshape(vectors, local_num, local_span, width),
            onehot,
            preferred_element_type=jnp.float32,
        ).astype(jnp.bfloat16)
        coarse = jnp.einsum(
            "vjkc,kcd->vjd", grouped, restrict[level_num], preferred_element_type=jnp.float32
        ) * span_blocks ** (-0.5)
        summed.append(coarse)
        kind_maps.append(pattern[level_num].reshape(local_num, local_span))
        groups.append(span_blocks // local_span)
        counts_list.append(coarse_num)
    crossing = [level_num for level_num in range(levels) if groups[level_num] > 1]
    stacked = jnp.stack([summed[level_num] for level_num in crossing])
    widest = max((groups[level_num] for level_num in crossing))
    for bit_num in range(widest.bit_length() - 1):
        first = min(
            (
                position
                for position in range(len(crossing))
                if groups[crossing[position]] > 2**bit_num
            )
        )
        upper = stacked[first:]
        partner = partner_2(upper, "gx", bit_num)
        stacked = jnp.concatenate([stacked[:first], upper + partner], axis=0)
    for position in range(len(crossing)):
        summed[crossing[position]] = stacked[position]
    for level_num in range(levels):
        rounded = summed[level_num].astype(jnp.bfloat16)
        solved = jnp.einsum(
            "vjd,de->vje", rounded, coarse_inv[level_num], preferred_element_type=jnp.float32
        ).astype(jnp.bfloat16)
        lifted = jnp.einsum(
            "vjd,kcd->vjkc", solved, restrict[level_num], preferred_element_type=jnp.float32
        )
        kind_map = kind_maps[level_num]
        for kind_num in range(kind_count):
            chosen = (kind_map == kind_num)[None, :, :, None]
            part_add = jnp.where(chosen, lifted[:, :, kind_num][:, :, None, :], jnp.float32(0.0))
            result = result + part_add.reshape(vectors, blocks, width)
    return result


def solution(mesh):
    in_specs = (P(None, "gx", None), P(None, "gx"), P(), P(), P())
    out_specs = P(None, "gx", None)
    return jax.shard_map(shards, mesh=mesh, in_specs=in_specs, out_specs=out_specs, check_vma=False)
```

profile of v0, /device:TPU:0, one launch (start us, length us, event | category | flops | bytes accessed | tf_op | source)
XLA Modules:
  0.0 162.0 jit_solution(2426209345188751192)
XLA Ops:
  1.8 6.4 %collective-permute-start.1 = (bf16[64,1,128]{2,1,0:T(2,128)(2,1)}, bf16[64,1,128]{2,1,0:T(2,128)(2,1)}, u32[]{:S(2)}, u32[]{:S(2)}) collective-permute-start(bf16[64,1,128]{2,1,0:T(2,128)(2,1)} %get-tuple-element.44), channel_id=1, source_target_pairs={{1,0},{2,1},{3,2},{4,3},{5,4},{6,5},{7,6},{8,7},{9,8},{10,9},{11,1... | collective-permute-start | bytes 49160 | tf_op jit(solution)/shard_map/ppermute | solution.py:16
  9.2 2.8 %fusion.52 = bf16[64,4,128]{2,1,0:T(4,128)(2,1)S(1)} fusion(bf16[64,256,128]{2,1,0:T(8,128)(2,1)} %param.5, s32[256]{0:T(256)S(1)} %bitcast.462), kind=kOutput, calls=%fused_computation.82 | convolution fusion | flops 16811008 | bytes 4260864 | tf_op jit(solution)/shard_map/vjsc,jsk->vjkc/dot_general | solution.py:55
  12.1 2.8 %fusion.51 = bf16[64,4,128]{2,1,0:T(4,128)(2,1)S(1)} fusion(bf16[64,256,128]{2,1,0:T(8,128)(2,1)} %param.5, s32[256]{0:T(256)S(1)} %bitcast.461), kind=kOutput, calls=%fused_computation.81 | convolution fusion | flops 16811008 | bytes 4260864 | tf_op jit(solution)/shard_map/vjsc,jsk->vjkc/dot_general | solution.py:55
  18.5 2.8 %fusion.50 = bf16[64,4,128]{2,1,0:T(4,128)(2,1)S(1)} fusion(bf16[64,256,128]{2,1,0:T(8,128)(2,1)} %param.5, s32[256]{0:T(256)S(1)} %bitcast.458), kind=kOutput, calls=%fused_computation.80 | convolution fusion | flops 16811008 | bytes 4260864 | tf_op jit(solution)/shard_map/vjsc,jsk->vjkc/dot_general | solution.py:55
  22.5 3.0 %fusion.33 = bf16[4,4,64,128]{3,1,2,0:T(4,128)(2,1)S(1)} fusion(bf16[64,4,64,128]{3,2,1,0:T(8,128)(2,1)} %bitcast.448, s32[4,64]{1,0:T(4,128)S(1)} %eq.383), kind=kOutput, calls=%fused_computation.44 | convolution fusion | flops 16778240 | bytes 4457472 | tf_op jit(solution)/shard_map/vjsc,jsk->vjkc/dot_general | solution.py:55
  27.7 3.1 %fusion.35 = bf16[16,4,64,128]{3,1,2,0:T(4,128)(2,1)S(1)} fusion(bf16[64,16,16,128]{3,2,1,0:T(8,128)(2,1)} %bitcast.449, s32[16,16]{1,0:T(8,128)S(1)} %eq.371), kind=kOutput, calls=%fused_computation.46 | convolution fusion | flops 16778240 | bytes 5243904 | tf_op jit(solution)/shard_map/vjsc,jsk->vjkc/dot_general | solution.py:55
  34.2 5.6 %fusion.39 = bf16[64,4,64,128]{3,1,2,0:T(4,128)(2,1)S(1)} fusion(bf16[64,64,4,128]{3,2,1,0:T(4,128)(2,1)} %bitcast.450, s32[64,4]{1,0:T(8,128)S(1)} %copy-done.18), kind=kOutput, calls=%fused_computation.50 | convolution fusion | flops 16778240 | bytes 8389632 | tf_op jit(solution)/shard_map/vjsc,jsk->vjkc/dot_general | solution.py:55
  39.8 3.2 %copy.82 = bf16[64,4,64,128]{3,2,1,0:T(8,128)(2,1)} copy(bf16[64,4,64,128]{3,1,2,0:T(4,128)(2,1)S(1)} %fusion.39) | data formatting | bytes 8388608 | tf_op jit(solution)/shard_map/vjsc,jsk->vjkc/dot_general | solution.py:55
  43.1 8.1 %fusion.44 = bf16[64,64,128,1]{2,1,3,0:T(8,128)(2,1)} fusion(bf16[64,64,4,128]{3,0,2,1:T(8,128)(2,1)} %bitcast.455, bf16[8,4,128,128]{3,2,1,0:T(8,128)(2,1)S(1)} %copy-done.2, bf16[8,128,128]{2,1,0:T(8,128)(2,1)} %param.9), kind=kOutput, calls=%fused_computation.60 | convolution fusion | flops 672661504 | bytes 5406720 | tf_op jit(solution)/shard_map/vjd,de->vje/dot_general | solution.py:86
  51.2 2.5 %fusion.96 = f32[64,64,4,128]{3,1,2,0:T(8,128)S(1)} fusion(bf16[64,64,128,1]{2,1,3,0:T(8,128)(2,1)} %fusion.44, bf16[8,4,128,128]{3,2,1,0:T(8,128)(2,1)S(1)} %copy-done.2), kind=kOutput, calls=%fused_computation.140 | convolution fusion | flops 536870912 | bytes 9568256 | tf_op jit(solution)/shard_map/vjd,kcd->vjkc/dot_general | solution.py:89
  53.7 3.3 %slice_bitcast_fusion.3 = (f32[64,64,128]{2,1,0:T(8,128)}, f32[64,64,128]{2,1,0:T(8,128)}, f32[64,64,128]{2,1,0:T(8,128)}, f32[64,64,128]{2,1,0:T(8,128)S(1)}) fusion(f32[64,64,4,128]{3,1,2,0:T(8,128)S(1)} %fusion.96), kind=kLoop, calls=%fused_computation.55 | loop fusion | bytes 16777216 | tf_op jit(solution)/shard_map/jit(_where)/broadcast_in_dim | solution.py:95
  58.1 4.5 %fusion.150 = f32[64,256,128]{2,1,0:T(8,128)} fusion(bf16[64,256,128]{2,1,0:T(8,128)(2,1)S(1)} %copy-done.1, bf16[3,128,128]{2,1,0:T(8,128)(2,1)S(1)} %copy-done.16), kind=kOutput, calls=%fused_computation.207 | convolution fusion | flops 536870912 | bytes 12615680 | tf_op jit(solution)/shard_map/vic,cd->vid/dot_general | solution.py:37
  65.8 5.2 %fusion.31 = f32[64,256,128]{2,1,0:T(8,128)} fusion(bf16[64,256,128]{2,1,0:T(8,128)(2,1)S(1)} %copy-done.1, bf16[64,1,128]{2,1,0:T(2,128)(2,1)} %collective-permute-done, bf16[3,128,128]{2,1,0:T(8,128)(2,1)S(1)} %copy-done.16), kind=kOutput, calls=%fused_computation.42 | convolution fusion | flops 545259520 | bytes 12632064 | tf_op jit(solution)/shard_map/vic,cd->vid/dot_general | solution.py:34
  74.0 1.8 %convolution_bitcast_fusion.4 = f32[64,1,4,128]{3,0,2,1:T(8,128)} fusion(bf16[8,4,128,128]{3,2,1,0:T(8,128)(2,1)} %param.8, bf16[8,128,128]{2,1,0:T(8,128)(2,1)} %param.9, f32[4,64,1,128]{3,1,2,0:T(8,128)S(1)} %fusion.208), kind=kOutput, calls=%fused_computation.70 | convolution fusion | flops 10493952 | bytes 311296 | tf_op jit(solution)/shard_map/vjd,kcd->vjkc/dot_general | solution.py:89
  75.8 2.3 %collective-permute-done.4 = f32[3,64,1,128]{3,1,2,0:T(8,128)} collective-permute-done((f32[3,64,1,128]{3,1,2,0:T(8,128)}, f32[3,64,1,128]{3,1,2,0:T(8,128)}, u32[]{:S(2)}, u32[]{:S(2)}) %collective-permute-start.4) | collective-permute-done | bytes 98336 | tf_op jit(solution)/shard_map/ppermute | solution.py:24
  81.0 2.7 %collective-permute-done.5 = f32[3,64,1,128]{3,1,2,0:T(8,128)S(1)} collective-permute-done((f32[3,64,1,128]{3,1,2,0:T(8,128)S(1)}, f32[3,64,1,128]{3,1,2,0:T(8,128)S(1)}, u32[]{:S(2)}, u32[]{:S(2)}) %collective-permute-start.5) | collective-permute-done | bytes 98336 | tf_op jit(solution)/shard_map/ppermute | solution.py:24
  84.4 1.8 %convolution_bitcast_fusion.3 = f32[64,1,4,128]{3,0,2,1:T(8,128)} fusion(bf16[8,4,128,128]{3,2,1,0:T(8,128)(2,1)} %param.8, bf16[8,128,128]{2,1,0:T(8,128)(2,1)} %param.9, f32[3,64,1,128]{3,1,2,0:T(8,128)S(1)} %add.142), kind=kOutput, calls=%fused_computation.69 | convolution fusion | flops 10493952 | bytes 311296 | tf_op jit(solution)/shard_map/vjd,kcd->vjkc/dot_general | solution.py:89
  86.2 2.8 %collective-permute-start.6 = (f32[2,64,1,128]{3,1,2,0:T(8,128)}, f32[2,64,1,128]{3,1,2,0:T(8,128)S(1)}, u32[]{:S(2)}, u32[]{:S(2)}) collective-permute-start(f32[2,64,1,128]{3,1,2,0:T(8,128)} %slice.330), channel_id=1, source_target_pairs={{0,16},{1,17},{2,18},{3,19},{4,20},{5,21},{6,22},{7,23},{8,24},{9,... | collective-permute-start | bytes 196616 | tf_op jit(solution)/shard_map/ppermute | solution.py:24
  93.4 1.9 %convolution_bitcast_fusion.2 = f32[64,1,4,128]{3,0,2,1:T(8,128)} fusion(bf16[8,4,128,128]{3,2,1,0:T(8,128)(2,1)} %param.8, bf16[8,128,128]{2,1,0:T(8,128)(2,1)} %param.9, bf16[2,64,1,128]{3,1,2,0:T(8,128)(2,1)} %add_convert_fusion), kind=kOutput, calls=%fused_computation.68 | convolution fusion | flops 10493952 | bytes 311296 | tf_op jit(solution)/shard_map/vjd,kcd->vjkc/dot_general | solution.py:89
  96.8 6.6 %broadcast_in_dim.552 = f32[64,64,4,128]{3,2,1,0:T(4,128)} broadcast(f32[64,64,128]{2,1,0:T(8,128)} %get-tuple-element.40), dimensions={0,1,3} | broadcast | bytes 10485760 | tf_op jit(solution)/shard_map/jit(_where)/broadcast_in_dim | solution.py:95
  103.4 6.5 %broadcast_in_dim.565 = f32[64,64,4,128]{3,2,1,0:T(4,128)} broadcast(f32[64,64,128]{2,1,0:T(8,128)} %get-tuple-element.41), dimensions={0,1,3} | broadcast | bytes 10485760 | tf_op jit(solution)/shard_map/jit(_where)/broadcast_in_dim | solution.py:95
  109.9 6.4 %broadcast_in_dim.561 = f32[64,64,4,128]{3,2,1,0:T(4,128)} broadcast(f32[64,64,128]{2,1,0:T(8,128)} %get-tuple-element.42), dimensions={0,1,3} | broadcast | bytes 10485760 | tf_op jit(solution)/shard_map/jit(_where)/broadcast_in_dim | solution.py:95
  116.3 4.8 %broadcast_in_dim.557 = f32[64,64,4,128]{3,2,1,0:T(4,128)} broadcast(f32[64,64,128]{2,1,0:T(8,128)S(1)} %get-tuple-element.43), dimensions={0,1,3} | broadcast | bytes 10485760 | tf_op jit(solution)/shard_map/jit(_where)/broadcast_in_dim | solution.py:95
  121.1 40.7 %fusion.20 = f32[64,256,128]{2,1,0:T(8,128)} fusion(f32[64,256,128]{2,1,0:T(8,128)} %bitcast.452, f32[64,256,128]{2,1,0:T(8,128)} %bitcast.453, f32[64,256,128]{2,1,0:T(8,128)} %bitcast.454, f32[64,256,128]{2,1,0:T(8,128)} %bitcast.451, f32[64,256,128]{2,1,0:T(8,128)} %fusion.31, f32[64,256,128]{2,1,0:T(8,128)} %fusion.150, ...), kind=kOutput, calls=%fused_computation.21 | convolution fusion | flops 683671552 | bytes 66272256 | tf_op jit(solution)/shard_map/vic,cd->vid/dot_general | solution.py:40
  (87 shorter events, 29.8 us)
Async XLA Ops:
  0.0 15.2 %copy-start = (bf16[64,256,128]{2,1,0:T(8,128)(2,1)S(1)}, bf16[64,256,128]{2,1,0:T(8,128)(2,1)}, u32[]{:S(2)}) copy-start(bf16[64,256,128]{2,1,0:T(8,128)(2,1)} %param.5) | copy-start | bytes 12582916
  0.0 14.9 %copy-start.2 = (bf16[8,4,128,128]{3,2,1,0:T(8,128)(2,1)S(1)}, bf16[8,4,128,128]{3,2,1,0:T(8,128)(2,1)}, u32[]{:S(2)}) copy-start(bf16[8,4,128,128]{3,2,1,0:T(8,128)(2,1)} %param.8) | copy-start | bytes 3145732
  1.8 95.0 %collective-permute-start.1 = (bf16[64,1,128]{2,1,0:T(2,128)(2,1)}, bf16[64,1,128]{2,1,0:T(2,128)(2,1)}, u32[]{:S(2)}, u32[]{:S(2)}) collective-permute-start(bf16[64,1,128]{2,1,0:T(2,128)(2,1)} %get-tuple-element.44), channel_id=1, source_target_pairs={{1,0},{2,1},{3,2},{4,3},{5,4},{6,5},{7,6},{8,7},{9,8},{10,9},{11,1... | collective-permute-start | bytes 49160 | tf_op jit(solution)/shard_map/ppermute | solution.py:16
  8.2 57.6 %collective-permute-start = (bf16[64,1,128]{2,1,0:T(2,128)(2,1)}, bf16[64,1,128]{2,1,0:T(2,128)(2,1)}, u32[]{:S(2)}, u32[]{:S(2)}) collective-permute-start(bf16[64,1,128]{2,1,0:T(2,128)(2,1)} %get-tuple-element.45), channel_id=1, source_target_pairs={{0,1},{1,2},{2,3},{3,4},{4,5},{5,6},{6,7},{7,8},{8,9},{9,10},{10,1... | collective-permute-start | bytes 49160 | tf_op jit(solution)/shard_map/ppermute | solution.py:14
  15.1 1.8 %copy-start.8 = (f32[1,64,1,128]{3,1,2,0:T(8,128)}, f32[1,64,1,128]{3,1,2,0:T(8,128)S(1)}, u32[]{:S(2)}) copy-start(f32[1,64,1,128]{3,1,2,0:T(8,128)S(1)} %fusion.60) | copy-start | bytes 98308
  15.2 2.3 %copy-start.10 = (f32[1,64,1,128]{3,1,2,0:T(8,128)}, f32[1,64,1,128]{3,1,2,0:T(8,128)S(1)}, u32[]{:S(2)}) copy-start(f32[1,64,1,128]{3,1,2,0:T(8,128)S(1)} %fusion.62) | copy-start | bytes 98308
  17.6 48.1 %collective-permute-start.2 = (f32[4,64,1,128]{3,1,2,0:T(8,128)}, f32[4,64,1,128]{3,1,2,0:T(8,128)S(1)}, u32[]{:S(2)}, u32[]{:S(2)}) collective-permute-start(f32[4,64,1,128]{3,1,2,0:T(8,128)} %pad_maximum_fusion.6), channel_id=1, source_target_pairs={{0,1},{1,0},{2,3},{3,2},{4,5},{5,4},{6,7},{7,6},{8,9},{9,8},{10,11... | collective-permute-start | bytes 393224 | tf_op jit(solution)/shard_map/ppermute | solution.py:24
  27.6 6.6 %copy-start.18 = (s32[64,4]{1,0:T(8,128)S(1)}, s32[64,4]{1,0:T(8,128)}, u32[]{:S(2)}) copy-start(s32[64,4]{1,0:T(8,128)} %eq.356) | copy-start | bytes 3076
  53.6 4.4 %copy-start.1 = (bf16[64,256,128]{2,1,0:T(8,128)(2,1)S(1)}, bf16[64,256,128]{2,1,0:T(8,128)(2,1)}, u32[]{:S(2)}) copy-start(bf16[64,256,128]{2,1,0:T(8,128)(2,1)} %param.5) | copy-start | bytes 12582916
  53.6 4.4 %copy-start.16 = (bf16[3,128,128]{2,1,0:T(8,128)(2,1)S(1)}, bf16[3,128,128]{2,1,0:T(8,128)(2,1)}, u32[]{:S(2)}) copy-start(bf16[3,128,128]{2,1,0:T(8,128)(2,1)} %param.7) | copy-start | bytes 294916
  58.0 5.3 %copy-start.7 = (f32[64,4,128]{2,0,1:T(8,128)S(1)}, f32[64,4,128]{2,0,1:T(8,128)}, u32[]{:S(2)}) copy-start(f32[64,4,128]{2,0,1:T(8,128)} %get-tuple-element.51) | copy-start | bytes 393220
  58.0 5.4 %copy-start.6 = (f32[64,4,128]{2,0,1:T(8,128)S(1)}, f32[64,4,128]{2,0,1:T(8,128)}, u32[]{:S(2)}) copy-start(f32[64,4,128]{2,0,1:T(8,128)} %get-tuple-element.52) | copy-start | bytes 393220
  58.0 6.1 %copy-start.5 = (f32[64,4,128]{2,0,1:T(8,128)S(1)}, f32[64,4,128]{2,0,1:T(8,128)}, u32[]{:S(2)}) copy-start(f32[64,4,128]{2,0,1:T(8,128)} %get-tuple-element.53) | copy-start | bytes 393220
  58.0 6.8 %copy-start.17 = (s32[8,256]{1,0:T(8,128)S(1)}, s32[8,256]{1,0:T(8,128)}, u32[]{:S(2)}) copy-start(s32[8,256]{1,0:T(8,128)} %param.6) | copy-start | bytes 24580
  58.1 7.6 %copy-start.9 = (f32[1,64,1,128]{3,1,2,0:T(8,128)S(1)}, f32[1,64,1,128]{3,1,2,0:T(8,128)}, u32[]{:S(2)}) copy-start(f32[1,64,1,128]{3,1,2,0:T(8,128)} %copy-done.8) | copy-start | bytes 98308
  58.1 7.6 %copy-start.11 = (f32[1,64,1,128]{3,1,2,0:T(8,128)S(1)}, f32[1,64,1,128]{3,1,2,0:T(8,128)}, u32[]{:S(2)}) copy-start(f32[1,64,1,128]{3,1,2,0:T(8,128)} %copy-done.10) | copy-start | bytes 98308
  58.1 7.5 %copy-start.13 = (f32[1,64,1,128]{3,1,2,0:T(8,128)S(1)}, f32[1,64,1,128]{3,1,2,0:T(8,128)}, u32[]{:S(2)}) copy-start(f32[1,64,1,128]{3,1,2,0:T(8,128)} %copy-done.12) | copy-start | bytes 98308
  58.1 7.5 %copy-start.15 = (f32[1,64,1,128]{3,1,2,0:T(8,128)S(1)}, f32[1,64,1,128]{3,1,2,0:T(8,128)}, u32[]{:S(2)}) copy-start(f32[1,64,1,128]{3,1,2,0:T(8,128)} %copy-done.14) | copy-start | bytes 98308
  65.6 5.4 %copy-start.4 = (f32[4,64,1,128]{3,1,2,0:T(8,128)}, f32[4,64,1,128]{3,1,2,0:T(8,128)S(1)}, u32[]{:S(2)}) copy-start(f32[4,64,1,128]{3,1,2,0:T(8,128)S(1)} %collective-permute-done.2) | copy-start | bytes 393220
  65.7 6.0 %collective-permute-start.3 = (f32[4,64,1,128]{3,1,2,0:T(8,128)S(1)}, f32[4,64,1,128]{3,1,2,0:T(8,128)S(1)}, u32[]{:S(2)}, u32[]{:S(2)}) collective-permute-start(f32[4,64,1,128]{3,1,2,0:T(8,128)S(1)} %fusion.196), channel_id=1, source_target_pairs={{0,2},{1,3},{2,0},{3,1},{4,6},{5,7},{6,4},{7,5},{8,10},{9,11},{10,... | collective-permute-start | bytes 393224 | tf_op jit(solution)/shard_map/ppermute | solution.py:24
  73.2 4.9 %collective-permute-start.4 = (f32[3,64,1,128]{3,1,2,0:T(8,128)}, f32[3,64,1,128]{3,1,2,0:T(8,128)}, u32[]{:S(2)}, u32[]{:S(2)}) collective-permute-start(f32[3,64,1,128]{3,1,2,0:T(8,128)} %slice.324), channel_id=1, source_target_pairs={{0,4},{1,5},{2,6},{3,7},{4,0},{5,1},{6,2},{7,3},{8,12},{9,13},{10,... | collective-permute-start | bytes 294920 | tf_op jit(solution)/shard_map/ppermute | solution.py:24
  79.1 4.7 %collective-permute-start.5 = (f32[3,64,1,128]{3,1,2,0:T(8,128)S(1)}, f32[3,64,1,128]{3,1,2,0:T(8,128)S(1)}, u32[]{:S(2)}, u32[]{:S(2)}) collective-permute-start(f32[3,64,1,128]{3,1,2,0:T(8,128)S(1)} %slice_add_fusion), channel_id=1, source_target_pairs={{0,8},{1,9},{2,10},{3,11},{4,12},{5,13},{6,14},{7,15},{8,0},{9,1},... | collective-permute-start | bytes 294920 | tf_op jit(solution)/shard_map/ppermute | solution.py:24
  86.2 5.4 %collective-permute-start.6 = (f32[2,64,1,128]{3,1,2,0:T(8,128)}, f32[2,64,1,128]{3,1,2,0:T(8,128)S(1)}, u32[]{:S(2)}, u32[]{:S(2)}) collective-permute-start(f32[2,64,1,128]{3,1,2,0:T(8,128)} %slice.330), channel_id=1, source_target_pairs={{0,16},{1,17},{2,18},{3,19},{4,20},{5,21},{6,22},{7,23},{8,24},{9,... | collective-permute-start | bytes 196616 | tf_op jit(solution)/shard_map/ppermute | solution.py:24
  109.9 11.2 %copy-start.3 = (f32[64,4,128]{2,1,0:T(4,128)S(1)}, f32[64,4,128]{2,1,0:T(4,128)}, u32[]{:S(2)}) copy-start(f32[64,4,128]{2,1,0:T(4,128)} %copy.16) | copy-start | bytes 393220
  (2 other events, 2.2 us)
where the time goes:
time: 163 us; the launch traced here: 162 us
  matrix products  94.4 us (58%)
  local copies, waits for them, and re-layouts  45.9 us (28%)
  starting transfers between devices  10.6 us (7%)
  waiting for transfers between devices  6.77 us (4%)
  other arithmetic  3.87 us (2%)
    dot_general x1, matrix products, shards(): jnp.einsum('vic,cd->vid', padded[:, 2:], stencil[2], preferred_element_ty...  40.7 us
    broadcast_in_dim x15, local copies, waits for them, and re-layouts, shards(): jnp.where(chosen, lifted[:, :, kind_num][:, :, None, :], jnp.float32(0.0))  36.2 us
    dot_general x8, matrix products, shards(): jnp.einsum('vjsc,jsk->vjkc', fine.reshape(vectors, local_num, local_span,...  21.4 us
    dot_general x8, matrix products, shards(): jnp.einsum('vjd,kcd->vjkc', solved, restrict[level_num], preferred_elemen...  10.9 us
    dot_general x3, matrix products, shards(): jnp.einsum('vjd,de->vje', rounded, coarse_inv[level_num], preferred_eleme...  10.8 us
    ppermute x5, waiting for transfers between devices, partner_2(): lax.ppermute(x, axis, [(i, i ^ 1 << apart) for i in range(lax.axis_size(a...  6.76 us
    ppermute x1, starting transfers between devices, padded_2(): lax.ppermute(head, axis, [((i + 1) % count, i) for i in range(count)])  6.4 us
    dot_general x1, matrix products, shards(): jnp.einsum('vic,cd->vid', padded[:, :-2], stencil[0], preferred_element_t...  5.23 us
  transfers between devices with their start and end apart: 7, of which 4 were waited for; matrix products, arithmetic and copies ran while one was open for 47% of the time, Pallas kernels for 0%

commit v1 on v0

v1 whole, which is shorter than its diff:
```python
import functools

import jax
import jax.numpy as jnp
from jax import lax
from jax.experimental import pallas as pl
from jax.experimental.pallas import tpu as pltpu
from jax.sharding import PartitionSpec as P

BF = jnp.bfloat16
F32 = jnp.float32
MIB = 1 << 20


def dot(a, b):
    return jnp.dot(a, b, preferred_element_type=F32)


def vmem_spec():
    return pl.BlockSpec(memory_space=pltpu.VMEM)


def any_spec():
    return pl.BlockSpec(memory_space=pltpu.HBM)


class Plan:
    def __init__(self, devices, fine, pattern, restrict):
        self.devices = devices
        self.nv, self.blocks, self.width = fine.shape
        self.levels, self.kinds = restrict.shape[:2]
        total = self.blocks * devices
        self.spans = []
        for level in range(self.levels):
            self.spans.append(total // max(total // 4 ** (level + 1), 1))
        self.runs = [self.blocks // min(s, self.blocks) for s in self.spans]
        local = [l for l in range(self.levels) if self.spans[l] <= self.blocks]
        self.top = [l for l in range(self.levels) if self.spans[l] > self.blocks]
        self.wide = [l for l in local if self.runs[l] * self.kinds == self.blocks]
        self.mid = [l for l in local if l not in self.wide and self.runs[l] % 16 == 0]
        self.thin = [l for l in local if l not in self.wide and l not in self.mid]
        self.row = {}
        at = 0
        for l in self.mid:
            self.row[l] = at
            at += self.kinds * self.runs[l]
        self.mid_rows = at
        at = 0
        for l in self.thin + self.top:
            self.row[l] = at
            at += self.kinds * self.runs[l]
        self.first_row = at
        self.last_row = at + 1
        self.thin_rows = -(-(at + 2) // 8) * 8
        self.a_rows = -(-(self.mid_rows + self.thin_rows) // 16) * 16
        self.col = {}
        at = 0
        for l in self.mid + self.thin:
            self.col[l] = at
            at += self.kinds * self.runs[l]
        self.cols = -(-at // 128) * 128
        self.used_cols = at
        self.top_cols = self.kinds * len(self.top)

    def target(self, pat, l, base):
        index = lax.broadcasted_iota(jnp.int32, (1, self.blocks), 1)
        run = index // min(self.spans[l], self.blocks)
        return base + pat[l : l + 1, :] * self.runs[l] + run


def kernel_a(plan, fine, pattern, restrict_hbm, fine_v, g_mid, g_thin, tops, msg, hb, m1, mt1, mt2, mtop, pat_s, r_s, m_s, sems, psem, rsem):
    nv, blocks, width = plan.nv, plan.blocks, plan.width
    kinds = plan.kinds
    chunks = sems.shape[0]
    per = nv // chunks
    ntop = len(plan.top)
    pcopy = pltpu.make_async_copy(pattern, pat_s, psem)
    pcopy.start()
    copies = [
        pltpu.make_async_copy(fine.at[pl.ds(n * per, per)], fine_v.at[pl.ds(n * per, per)], sems.at[n])
        for n in range(chunks)
    ]
    for c in copies:
        c.start()
    rcopy = pltpu.make_async_copy(restrict_hbm.at[pl.ds(plan.top[0], ntop)], r_s, rsem)
    rcopy.start()
    pcopy.wait()
    pat = pat_s[...]
    rows = lax.broadcasted_iota(jnp.int32, (plan.a_rows, blocks), 0)
    hit = jnp.zeros((plan.a_rows, blocks), jnp.bool_)
    for l in plan.mid:
        hit = hit | (rows == plan.target(pat, l, plan.row[l]))
    for l in plan.thin + plan.top:
        hit = hit | (rows == plan.target(pat, l, plan.row[l] + plan.mid_rows))
    cols = lax.broadcasted_iota(jnp.int32, (plan.a_rows, blocks), 1)
    hit = hit | ((rows == plan.first_row + plan.mid_rows) & (cols == 0))
    hit = hit | ((rows == plan.last_row + plan.mid_rows) & (cols == blocks - 1))
    m_s[...] = jnp.where(hit, 1.0, 0.0).astype(BF)
    wide = plan.wide[0]
    t_wide = plan.target(pat, wide, 0)
    wrows = lax.broadcasted_iota(jnp.int32, (blocks, blocks), 0)
    m1[...] = jnp.where(wrows == t_wide, 1.0, 0.0).astype(BF)

    def column(row_vec, lanes):
        return jnp.broadcast_to(row_vec.astype(F32), (lanes, blocks)).T

    lane = lax.broadcasted_iota(jnp.int32, (blocks, 128), 1).astype(F32)
    tw = column(t_wide, 128)
    for n in range(blocks // 128):
        mt1[:, pl.ds(n * 128, 128)] = jnp.where(tw == lane + float(n * 128), 1.0, 0.0).astype(BF)
    hit2 = jnp.zeros((blocks, 128), jnp.bool_)
    for l in plan.mid + plan.thin:
        hit2 = hit2 | (column(plan.target(pat, l, plan.col[l]), 128) == lane)
    mt2[...] = jnp.where(hit2, 1.0, 0.0).astype(BF)
    hit3 = jnp.zeros((blocks, 128), jnp.bool_)
    for n, l in enumerate(plan.top):
        hit3 = hit3 | (column(pat[l : l + 1, :] + n * kinds, 128) == lane)
    mtop[...] = jnp.where(hit3, 1.0, 0.0).astype(BF)

    m = m_s[...]
    for n in range(chunks):
        copies[n].wait()
        for p in range(per // 2):
            v = n * per + 2 * p
            pair = jnp.concatenate([fine_v[v], fine_v[v + 1]], axis=1)
            g = dot(m, pair)
            for h in range(2):
                half = g[:, h * width : (h + 1) * width]
                for l in plan.mid:
                    runs = plan.runs[l]
                    for k in range(kinds):
                        r = plan.row[l] + k * runs
                        o = plan.row[l] * nv + k * runs * nv
                        g_mid[pl.ds(o + (v + h) * runs, runs), :] = half[r : r + runs].astype(BF)
                g_thin[pl.ds((v + h) * plan.thin_rows, plan.thin_rows), :] = half[
                    plan.mid_rows : plan.mid_rows + plan.thin_rows
                ]
    rcopy.wait()
    for n, l in enumerate(plan.top):
        parts = [
            g_thin[pl.ds(plan.row[l] + k, nv, stride=plan.thin_rows), :].astype(BF) for k in range(kinds)
        ]
        tile = jnp.concatenate([r_s[n, k] for k in range(kinds)], axis=0)
        coarse = dot(jnp.concatenate(parts, axis=1), tile)
        tops[n] = coarse
        msg[n] = coarse.astype(BF)
    first = g_thin[pl.ds(plan.first_row, nv, stride=plan.thin_rows), :].astype(BF)
    last = g_thin[pl.ds(plan.last_row, nv, stride=plan.thin_rows), :].astype(BF)
    odd = lax.axis_index("gx") % 2 == 1

    @pl.when(odd)
    def _():
        msg[ntop] = first
        hb[...] = last

    @pl.when(jnp.logical_not(odd))
    def _():
        msg[ntop] = last
        hb[...] = first


def chain(plan, l, parts, tiles, inverse, tiles_t):
    coarse = dot(jnp.concatenate(parts, axis=1), tiles) * plan.spans[l] ** (-0.5)
    solved = dot(coarse.astype(BF), inverse).astype(BF)
    return dot(solved, tiles_t)


def kernel_b1(plan, g_mid, g_thin, restrict, inverse, lsm):
    nv, kinds, width = plan.nv, plan.kinds, plan.width
    lv = plan.mid + plan.thin
    base = lv[0]
    lthin = g_thin
    for l in plan.mid:
        runs = plan.runs[l]
        o = plan.row[l] * nv
        tiles = jnp.concatenate([restrict[l, k] for k in range(kinds)], axis=0)
        tiles_t = jnp.concatenate([restrict[l, k].T for k in range(kinds)], axis=1)
        step = min(nv, 16)
        for s in range(0, nv, step):
            parts = [g_mid[pl.ds(o + (k * nv + s) * runs, step * runs), :] for k in range(kinds)]
            lifted = chain(plan, l, parts, tiles, inverse[l], tiles_t).astype(BF)
            for v in range(step):
                for k in range(kinds):
                    lsm[s + v, pl.ds(plan.col[l] + k * runs, runs), :] = lifted[
                        v * runs : (v + 1) * runs, k * width : (k + 1) * width
                    ]
    rows_at = plan.col[plan.thin[0]]
    blank = plan.cols - rows_at

    def body(scr):
        scr[...] = jnp.zeros_like(scr)
        for l in plan.thin:
            runs = plan.runs[l]
            tiles = jnp.concatenate([restrict[l, k] for k in range(kinds)], axis=0)
            tiles_t = jnp.concatenate([restrict[l, k].T for k in range(kinds)], axis=1)
            parts = []
            for k in range(kinds):
                rows = [
                    lthin[pl.ds(plan.row[l] + k * runs + j, nv, stride=plan.thin_rows), :].astype(BF)
                    for j in range(runs)
                ]
                parts.append(jnp.concatenate(rows, axis=0))
            lifted = chain(plan, l, parts, tiles, inverse[l], tiles_t)
            for j in range(runs):
                for k in range(kinds):
                    at = plan.col[l] - rows_at + k * runs + j
                    scr[pl.ds(at, nv, stride=blank), :] = lifted[
                        j * nv : (j + 1) * nv, k * width : (k + 1) * width
                    ]
        for v in range(nv):
            lsm[v, pl.ds(rows_at, blank), :] = scr[pl.ds(v * blank, blank), :].astype(BF)

    pl.run_scoped(body, pltpu.VMEM((nv * blank, width), F32))


def kernel_b(plan, start, count, fine_v, m1, mt1, mt2, lsm, stencil, restrict, inverse, out):
    kinds, width, blocks = plan.kinds, plan.width, plan.blocks
    l = plan.wide[0]
    runs = plan.runs[l]
    group = 4
    tiles = jnp.concatenate([restrict[l, k] for k in range(kinds)], axis=0)
    tiles_t = jnp.concatenate([restrict[l, k].T for k in range(kinds)], axis=1)
    zero = jnp.zeros((width, width), BF)
    sten = jnp.concatenate(
        [
            jnp.concatenate([stencil[1], stencil[0]], axis=1),
            jnp.concatenate([stencil[2], zero], axis=1),
        ],
        axis=0,
    )

    def body(scr, scr_t, scr_s):
        scr[...] = tiles
        scr_t[...] = tiles_t
        scr_s[...] = sten
        rowid = lax.broadcasted_iota(jnp.int32, (blocks, width), 0)

        def step(n, carry):
            v0 = start + n * group
            fs = [fine_v[v0 + q] for q in range(group)]
            gs = []
            for p in range(group // 2):
                pair = jnp.concatenate([fs[2 * p], fs[2 * p + 1]], axis=1)
                g = dot(m1[...], pair).astype(BF)
                gs.append(g[:, :width])
                gs.append(g[:, width:])
            parts = [
                jnp.concatenate([g[k * runs : (k + 1) * runs] for g in gs], axis=0) for k in range(kinds)
            ]
            lifted = chain(plan, l, parts, scr[...], inverse[l], scr_t[...]).astype(BF)
            for p in range(group // 2):
                halves = []
                for q in (2 * p, 2 * p + 1):
                    rows = [
                        lifted[q * runs : (q + 1) * runs, k * width : (k + 1) * width] for k in range(kinds)
                    ]
                    halves.append(jnp.concatenate(rows + [lsm[v0 + q]], axis=0))
                big = jnp.concatenate(halves, axis=1)
                e = dot(mt1[...], big[:blocks]) + dot(mt2[...], big[blocks:])
                for h in range(2):
                    q = 2 * p + h
                    f = fs[q].astype(F32)
                    nxt = jnp.where(rowid == blocks - 1, 0.0, pltpu.roll(f, blocks - 1, 0)).astype(BF)
                    y = dot(jnp.concatenate([fs[q], nxt], axis=1), scr_s[...])
                    prev = jnp.where(rowid == 0, 0.0, pltpu.roll(y[:, width:], 1, 0))
                    out[n * group + q] = e[:, h * width : (h + 1) * width] + y[:, :width] + prev
            return carry

        lax.fori_loop(0, count // group, step, 0)

    pl.run_scoped(
        body,
        pltpu.VMEM((kinds * width, width), BF),
        pltpu.VMEM((width, kinds * width), BF),
        pltpu.VMEM((2 * width, 2 * width), BF),
    )


def kernel_c(plan, counts, *refs):
    nparts = len(counts)
    res = refs[:nparts]
    sums, halo_r, halo_o, mtop, stencil, restrict, inverse, out = refs[nparts : nparts + 8]
    lt, h0, h2, ring, sems = refs[nparts + 8 :]
    nv, kinds, width, blocks = plan.nv, plan.kinds, plan.width, plan.blocks
    tcols = plan.top_cols
    for n, l in enumerate(plan.top):
        coarse = (sums[n] * plan.spans[l] ** (-0.5)).astype(BF)
        solved = dot(coarse, inverse[l]).astype(BF)
        tiles_t = jnp.concatenate([restrict[l, k].T for k in range(kinds)], axis=1)
        lifted = dot(solved, tiles_t)
        for k in range(kinds):
            lt[pl.ds(n * kinds + k, nv, stride=tcols), :] = lifted[:, k * width : (k + 1) * width]
    odd = lax.axis_index("gx") % 2 == 1
    hr = halo_r[...]
    ho = halo_o[...]
    h0[...] = dot(jnp.where(odd, hr, ho), stencil[0])
    h2[...] = dot(jnp.where(odd, ho, hr), stencil[2])
    slots, per = ring.shape[:2]
    mt = mtop[...][:, :tcols]

    total = 0
    for part in range(nparts):
        for n in range(counts[part] // per):
            slot = total % slots
            if total >= slots:
                pltpu.make_async_copy(ring.at[slot], out.at[pl.ds((total - slots) * per, per)], sems.at[slot]).wait()
            for p in range(per // 2):
                v = total * per + 2 * p
                pair = jnp.concatenate(
                    [lt[pl.ds(v * tcols, tcols), :], lt[pl.ds((v + 1) * tcols, tcols), :]], axis=1
                ).astype(BF)
                e = dot(mt, pair)
                for h in range(2):
                    ring[slot, 2 * p + h] = res[part][n * per + 2 * p + h] + e[:, h * width : (h + 1) * width]
                    ring[slot, 2 * p + h, pl.ds(0, 1), :] += h0[pl.ds(v + h, 1), :]
                    ring[slot, 2 * p + h, pl.ds(blocks - 1, 1), :] += h2[pl.ds(v + h, 1), :]
            pltpu.make_async_copy(ring.at[slot], out.at[pl.ds(total * per, per)], sems.at[slot]).start()
            total += 1
    for n in range(max(total - slots, 0), total):
        slot = n % slots
        pltpu.make_async_copy(ring.at[slot], out.at[pl.ds(n * per, per)], sems.at[slot]).wait()


def params(mib):
    return pltpu.CompilerParams(vmem_limit_bytes=mib * MIB)


def shards(fine, pattern, stencil, restrict, coarse_inv):
    devices = lax.axis_size("gx")
    plan = Plan(devices, fine, pattern, restrict)
    nv, blocks, width = fine.shape
    ntop = len(plan.top)
    chunks = 8
    vm = pltpu.VMEM
    a_out = (
        vm(fine.shape, BF),
        vm((plan.mid_rows * nv, width), BF),
        vm((plan.thin_rows * nv, width), F32),
        vm((ntop, nv, width), F32),
        vm((ntop + 1, nv, width), BF),
        vm((nv, width), BF),
        vm((blocks, blocks), BF),
        vm((blocks, blocks), BF),
        vm((blocks, 128), BF),
        vm((blocks, 128), BF),
    )
    fine_v, g_mid, g_thin, tops, msg, hb, m1, mt1, mt2, mtop = pl.pallas_call(
        functools.partial(kernel_a, plan),
        out_shape=a_out,
        in_specs=[any_spec(), any_spec(), any_spec()],
        out_specs=tuple(vmem_spec() for _ in a_out),
        scratch_shapes=[
            pltpu.VMEM(pattern.shape, jnp.int32),
            pltpu.VMEM((ntop,) + restrict.shape[1:], BF),
            pltpu.VMEM((plan.a_rows, blocks), BF),
            pltpu.SemaphoreType.DMA((chunks,)),
            pltpu.SemaphoreType.DMA,
            pltpu.SemaphoreType.DMA,
        ],
        compiler_params=params(12),
        name="gather_sums",
    )(fine, pattern, restrict)

    def permute(x, to):
        return lax.ppermute(x, "gx", [(i, to(i) % devices) for i in range(devices)])

    rounds = devices.bit_length() - 1
    halo_o = permute(hb, lambda i: i + 1 if i % 2 else i - 1)

    lsm = pl.pallas_call(
        functools.partial(kernel_b1, plan),
        out_shape=vm((nv, plan.cols, width), BF),
        in_specs=[vmem_spec()] * 4,
        out_specs=vmem_spec(),
        compiler_params=params(16),
        name="local_levels",
    )(g_mid, g_thin, restrict, coarse_inv)

    nparts = 4
    counts = [nv // nparts] * nparts
    parts = []
    for n in range(nparts):
        parts.append(
            pl.pallas_call(
                functools.partial(kernel_b, plan, sum(counts[:n]), counts[n]),
                out_shape=vm((counts[n], blocks, width), F32),
                in_specs=[vmem_spec()] * 8,
                out_specs=vmem_spec(),
                compiler_params=params(16),
                name="local_part",
            )(fine_v, m1, mt1, mt2, lsm, stencil, restrict, coarse_inv)
        )

    done = [None] * ntop
    live = tops
    alive = list(range(ntop))
    message = msg
    halo_r = None
    for b in range(rounds):
        flip = (1 << b) | 1
        got = permute(message, lambda i: i ^ flip)
        if b == 0:
            halo_r = got[ntop]
            got = got[:ntop]
        live = live + got.astype(F32)
        keep = [p for p in range(len(alive)) if plan.spans[plan.top[alive[p]]] // blocks > 2 << b]
        for p in range(len(alive)):
            if p not in keep:
                done[alive[p]] = live[p]
        if keep and len(keep) < len(alive):
            live = live[keep[0] :]
        alive = [alive[p] for p in keep]
        message = live.astype(BF)
    sums = jnp.stack(done)

    per = 4
    slots = 4
    return pl.pallas_call(
        functools.partial(kernel_c, plan, counts),
        out_shape=jax.ShapeDtypeStruct(fine.shape, F32),
        in_specs=[vmem_spec()] * (nparts + 7),
        out_specs=any_spec(),
        scratch_shapes=[
            pltpu.VMEM((plan.top_cols * nv, width), F32),
            pltpu.VMEM((nv, width), F32),
            pltpu.VMEM((nv, width), F32),
            pltpu.VMEM((slots, per, blocks, width), F32),
            pltpu.SemaphoreType.DMA((slots,)),
        ],
        compiler_params=params(16),
        name="finish",
    )(*parts, sums, halo_r, halo_o, mtop, stencil, restrict, coarse_inv)


def solution(mesh):
    in_specs = (P(None, "gx", None), P(None, "gx"), P(), P(), P())
    out_specs = P(None, "gx", None)
    return jax.shard_map(shards, mesh=mesh, in_specs=in_specs, out_specs=out_specs, check_vma=False)
```

time: 163 us -> 52.6 us (0.32)
  matrix products: 94.4 us -> 0 us
  local copies, waits for them, and re-layouts: 45.9 us -> 4.15 us
  Pallas kernels: 0 us -> 27.3 us
  other arithmetic: 3.87 us -> 0.09 us
  waiting for transfers between devices: 6.77 us -> 9.07 us
    dot_general x27 -> x0, matrix products: 94.4 us -> none  [the longest x1 40.7 us: shards(): jnp.einsum('vic,cd->vid', padded[:, 2:], stencil[2], preferred_element_ty...]
    broadcast_in_dim x15 -> x0, local copies, waits for them, and re-layouts: 36.2 us -> none  [shards(): jnp.where(chosen, lifted[:, :, kind_num][:, :, None, :], jnp.float32(0.0))]
    pallas_call x0 -> x7, Pallas kernels: none -> 27.3 us  [the longest x4 16.4 us: shards(): pl.pallas_call(functools.partial(kernel_b, plan, sum(counts[:n]), counts[...]
    slice x4, local copies, waits for them, and re-layouts: 4.06 us -> 0.03 us  [the longest x2 0.02 us: shards(): live = live[keep[0]:]]
    dot_general x2 -> x0, local copies, waits for them, and re-layouts: 3.5 us -> none  [shards(): jnp.einsum('vjsc,jsk->vjkc', fine.reshape(vectors, local_num, local_span,...]
    unnamed x39 -> x12, local copies, waits for them, and re-layouts: 1.24 us -> 4.12 us
    ppermute x7 -> x6, waiting for transfers between devices: 6.77 us -> 9.07 us  [permute(): return lax.ppermute(x, 'gx', [(i, to(i) % devices) for i in range(devices)])]
    add x4 -> x3, other arithmetic: 1.88 us -> 0.05 us  [shards(): live = live + got.astype(F32)]
  transfers between devices with their start and end apart: 7 -> 6, of which waited for: 4 -> 4; matrix products, arithmetic and copies ran while one was open for 47% -> 0% of each run, Pallas kernels for 0% -> 36%
where the time goes in v1:
time: 52.6 us; the launch traced here: 52.4 us
  Pallas kernels  27.3 us (52%)
  starting transfers between devices  11.6 us (22%)
  waiting for transfers between devices  9.07 us (17%)
  local copies, waits for them, and re-layouts  4.15 us (8%)
    pallas_call x4, Pallas kernels, shards(): pl.pallas_call(functools.partial(kernel_b, plan, sum(counts[:n]), counts[...  16.4 us
    ppermute x6, starting transfers between devices, permute(): return lax.ppermute(x, 'gx', [(i, to(i) % devices) for i in range(devices)])  11.6 us
    ppermute x6, waiting for transfers between devices, permute(): return lax.ppermute(x, 'gx', [(i, to(i) % devices) for i in range(devices)])  9.07 us
    pallas_call x1, Pallas kernels, shards(): pl.pallas_call(functools.partial(kernel_c, plan, counts), out_shape=jax.S...  5.4 us
    unnamed x12, local copies, waits for them, and re-layouts  4.12 us
    pallas_call x1, Pallas kernels, shards(): pl.pallas_call(functools.partial(kernel_a, plan), out_shape=a_out, in_spe...  2.89 us
    pallas_call x1, Pallas kernels, shards(): pl.pallas_call(functools.partial(kernel_b1, plan), out_shape=vm((nv, plan...  2.57 us
  transfers between devices with their start and end apart: 6, of which 4 were waited for; matrix products, arithmetic and copies ran while one was open for 0% of the time, Pallas kernels for 36%

profile of v1, /device:TPU:0, one launch (start us, length us, event | category | flops | bytes accessed | tf_op | source)
XLA Modules:
  0.0 52.4 jit_solution(5166425387100171428)
XLA Ops:
  0.0 1.2 %copy-done = bf16[8,4,128,128]{3,2,1,0:T(8,128)(2,1)S(1)} copy-done((bf16[8,4,128,128]{3,2,1,0:T(8,128)(2,1)S(1)}, bf16[8,4,128,128]{3,2,1,0:T(8,128)(2,1)}, u32[]{:S(2)}) %copy-start) | copy-done | bytes 1048600
  1.2 2.2 %copy-done.3 = bf16[64,256,128]{2,1,0:T(8,128)(2,1)S(1)} copy-done((bf16[64,256,128]{2,1,0:T(8,128)(2,1)S(1)}, bf16[64,256,128]{2,1,0:T(8,128)(2,1)}, u32[]{:S(2)}) %copy-start.3) | copy-done | bytes 4194328
  3.4 0.7 %copy-done.5 = s32[8,256]{1,0:T(8,128)S(1)} copy-done((s32[8,256]{1,0:T(8,128)S(1)}, s32[8,256]{1,0:T(8,128)}, u32[]{:S(2)}) %copy-start.5) | copy-done | bytes 8216
  4.1 2.9 %gather_sums.1 = (bf16[64,256,128]{2,1,0:T(8,128)(2,1)S(1)}, bf16[4096,128]{1,0:T(8,128)(2,1)S(1)}, f32[2560,128]{1,0:T(8,128)S(1)}, f32[4,64,128]{2,1,0:T(8,128...) custom-call(bf16[64,256,128]{2,1,0:T(8,128)(2,1)S(1)} %copy-done.3, ...), custom_call_target="tpu_custom_call" | custom-call | tf_op jit(solution)/shard_map/gather_sums/pallas_call | solution.py:347
  7.0 0.6 %collective-permute-start = (bf16[5,64,128]{2,1,0:T(8,128)(2,1)S(1)}, bf16[5,64,128]{2,1,0:T(8,128)(2,1)S(1)}, u32[]{:S(2)}, u32[]{:S(2)}) collective-permute-start(bf16[5,64,128]{2,1,0:T(8,128)(2,1)S(1)} %get-tuple-element.22), channel_id=1, source_target_pairs={{0,1},{1,0},{2,3},{3,2},{4,5},{5,4},{6,7},{7,6},{8,9},{9,8},{10,11... | collective-permute-start | bytes 245768 | tf_op jit(solution)/shard_map/ppermute | solution.py:365
  7.6 0.9 %collective-permute-done = bf16[5,64,128]{2,1,0:T(8,128)(2,1)S(1)} collective-permute-done((bf16[5,64,128]{2,1,0:T(8,128)(2,1)S(1)}, bf16[5,64,128]{2,1,0:T(8,128)(2,1)S(1)}, u32[]{:S(2)}, u32[]{:S(2)}) %collective-permute-start) | collective-permute-done | bytes 81952 | tf_op jit(solution)/shard_map/ppermute | solution.py:365
  8.5 2.7 %collective-permute-start.1 = (bf16[4,64,128]{2,1,0:T(8,128)(2,1)S(1)}, bf16[4,64,128]{2,1,0:T(8,128)(2,1)S(1)}, u32[]{:S(2)}, u32[]{:S(2)}) collective-permute-start(bf16[4,64,128]{2,1,0:T(8,128)(2,1)S(1)} %fusion), channel_id=1, source_target_pairs={{0,3},{1,2},{2,1},{3,0},{4,7},{5,6},{6,5},{7,4},{8,11},{9,10},{10,... | collective-permute-start | bytes 196616 | tf_op jit(solution)/shard_map/ppermute | solution.py:365
  11.2 2.2 %collective-permute-done.1 = bf16[4,64,128]{2,1,0:T(8,128)(2,1)S(1)} collective-permute-done((bf16[4,64,128]{2,1,0:T(8,128)(2,1)S(1)}, bf16[4,64,128]{2,1,0:T(8,128)(2,1)S(1)}, u32[]{:S(2)}, u32[]{:S(2)}) %collective-permute-start.1) | collective-permute-done | bytes 65568 | tf_op jit(solution)/shard_map/ppermute | solution.py:365
  13.4 2.0 %collective-permute-start.2 = (bf16[3,64,128]{2,1,0:T(8,128)(2,1)S(1)}, bf16[3,64,128]{2,1,0:T(8,128)(2,1)S(1)}, u32[]{:S(2)}, u32[]{:S(2)}) collective-permute-start(bf16[3,64,128]{2,1,0:T(8,128)(2,1)S(1)} %slice.44), channel_id=1, source_target_pairs={{0,5},{1,4},{2,7},{3,6},{4,1},{5,0},{6,3},{7,2},{8,13},{9,12},{10,... | collective-permute-start | bytes 147464 | tf_op jit(solution)/shard_map/ppermute | solution.py:365
  15.4 1.8 %collective-permute-done.2 = bf16[3,64,128]{2,1,0:T(8,128)(2,1)S(1)} collective-permute-done((bf16[3,64,128]{2,1,0:T(8,128)(2,1)S(1)}, bf16[3,64,128]{2,1,0:T(8,128)(2,1)S(1)}, u32[]{:S(2)}, u32[]{:S(2)}) %collective-permute-start.2) | collective-permute-done | bytes 49184 | tf_op jit(solution)/shard_map/ppermute | solution.py:365
  17.2 2.1 %collective-permute-start.3 = (bf16[3,64,128]{2,1,0:T(8,128)(2,1)S(1)}, bf16[3,64,128]{2,1,0:T(8,128)(2,1)S(1)}, u32[]{:S(2)}, u32[]{:S(2)}) collective-permute-start(bf16[3,64,128]{2,1,0:T(8,128)(2,1)S(1)} %fusion.1), channel_id=1, source_target_pairs={{0,9},{1,8},{2,11},{3,10},{4,13},{5,12},{6,15},{7,14},{8,1},{9,0},... | collective-permute-start | bytes 147464 | tf_op jit(solution)/shard_map/ppermute | solution.py:365
  19.3 4.2 %collective-permute-start.5 = (bf16[64,128]{1,0:T(8,128)(2,1)S(1)}, bf16[64,128]{1,0:T(8,128)(2,1)S(1)}, u32[]{:S(2)}, u32[]{:S(2)}) collective-permute-start(bf16[64,128]{1,0:T(8,128)(2,1)S(1)} %get-tuple-element.23), channel_id=1, source_target_pairs={{0,31},{1,2},{2,1},{3,4},{4,3},{5,6},{6,5},{7,8},{8,7},{9,10},{10,... | collective-permute-start | bytes 49160 | tf_op jit(solution)/shard_map/ppermute | solution.py:365
  23.5 2.6 %local_levels.1.lsm = bf16[64,128,128]{2,1,0:T(8,128)(2,1)S(1)} custom-call(bf16[4096,128]{1,0:T(8,128)(2,1)S(1)} %get-tuple-element.19.g_mid, f32[2560,128]{1,0:T(8,128)S(1)} %get-tuple-element.20.g_thin, bf16[8,4,128,128]{3,2,1,0:T(8,128)(2,1)S(1)} %copy-done, bf16[8,128,128]{2,1,0:T(8,128)(2,1)S(1)} %copy-done.2), custom_call_target="tpu_custom_call" | custom-call | tf_op jit(solution)/shard_map/local_levels/pallas_call | solution.py:370
  26.1 0.0 copy-done.1
  26.1 0.0 copy-done.4
  26.1 4.1 %local_part.7.refs_3_ = f32[16,256,128]{2,1,0:T(8,128)S(1)} custom-call(bf16[64,256,128]{2,1,0:T(8,128)(2,1)S(1)} %get-tuple-element.15.fine_v, bf16[256,256]{1,0:T(8,128)(2,1)S(1)} %get-tuple-element.16.m1, bf16[256,256]{1,0:T(8,128)(2,1)S(1)} %get-tuple-element.17.mt1, bf16[256,128]{1,0:T(8,128)(2,1)S(1)} %get-tuple-element.18.mt2, ...), custom_call_target="tpu_custom_call" | custom-call | tf_op jit(solution)/shard_map/local_part/pallas_call | solution.py:384
  30.2 4.1 %local_part.6.refs_2_ = f32[16,256,128]{2,1,0:T(8,128)S(1)} custom-call(bf16[64,256,128]{2,1,0:T(8,128)(2,1)S(1)} %get-tuple-element.15.fine_v, bf16[256,256]{1,0:T(8,128)(2,1)S(1)} %get-tuple-element.16.m1, bf16[256,256]{1,0:T(8,128)(2,1)S(1)} %get-tuple-element.17.mt1, bf16[256,128]{1,0:T(8,128)(2,1)S(1)} %get-tuple-element.18.mt2, ...), custom_call_target="tpu_custom_call" | custom-call | tf_op jit(solution)/shard_map/local_part/pallas_call | solution.py:384
  34.4 4.1 %local_part.5.refs_1_ = f32[16,256,128]{2,1,0:T(8,128)S(1)} custom-call(bf16[64,256,128]{2,1,0:T(8,128)(2,1)S(1)} %get-tuple-element.15.fine_v, bf16[256,256]{1,0:T(8,128)(2,1)S(1)} %get-tuple-element.16.m1, bf16[256,256]{1,0:T(8,128)(2,1)S(1)} %get-tuple-element.17.mt1, bf16[256,128]{1,0:T(8,128)(2,1)S(1)} %get-tuple-element.18.mt2, ...), custom_call_target="tpu_custom_call" | custom-call | tf_op jit(solution)/shard_map/local_part/pallas_call | solution.py:384
  38.5 4.1 %local_part.4.refs_0_ = f32[16,256,128]{2,1,0:T(8,128)S(1)} custom-call(bf16[64,256,128]{2,1,0:T(8,128)(2,1)S(1)} %get-tuple-element.15.fine_v, bf16[256,256]{1,0:T(8,128)(2,1)S(1)} %get-tuple-element.16.m1, bf16[256,256]{1,0:T(8,128)(2,1)S(1)} %get-tuple-element.17.mt1, bf16[256,128]{1,0:T(8,128)(2,1)S(1)} %get-tuple-element.18.mt2, ...), custom_call_target="tpu_custom_call" | custom-call | tf_op jit(solution)/shard_map/local_part/pallas_call | solution.py:384
  42.6 0.0 collective-permute-done.3
  42.6 0.1 collective-permute-start.4
  42.7 4.2 %collective-permute-done.4 = bf16[2,64,128]{2,1,0:T(8,128)(2,1)S(1)} collective-permute-done((bf16[2,64,128]{2,1,0:T(8,128)(2,1)S(1)}, bf16[2,64,128]{2,1,0:T(8,128)(2,1)S(1)}, u32[]{:S(2)}, u32[]{:S(2)}) %collective-permute-start.4) | collective-permute-done | bytes 32800 | tf_op jit(solution)/shard_map/ppermute | solution.py:365
  47.0 0.0 collective-permute-done.5.refs_6_
  47.0 5.4 %finish.1 = f32[64,256,128]{2,1,0:T(8,128)} custom-call(f32[16,256,128]{2,1,0:T(8,128)S(1)} %local_part.4.refs_0_, f32[16,256,128]{2,1,0:T(8,128)S(1)} %local_part.5.refs_1_, f32[16,256,128]{2,1,0:T(8,128)S(1)} %local_part.6.refs_2_, f32[16,256,128]{2,1,0:T(8,128)S(1)} %local_part.7.refs_3_, f32[4,64,128]{2,1,0:T(8,128)S(1)} %pad_maximum_fusion.refs_4_, ...), custom_call_target="tpu_custom_call" | custom-call | tf_op jit(solution)/shard_map/finish/pallas_call | solution.py:418
  (18 shorter events, 0.1 us)
Async XLA Ops:
  0.0 1.2 %copy-start = (bf16[8,4,128,128]{3,2,1,0:T(8,128)(2,1)S(1)}, bf16[8,4,128,128]{3,2,1,0:T(8,128)(2,1)}, u32[]{:S(2)}) copy-start(bf16[8,4,128,128]{3,2,1,0:T(8,128)(2,1)} %refs_9_.1) | copy-start | bytes 3145732
  1.2 2.2 %copy-start.3 = (bf16[64,256,128]{2,1,0:T(8,128)(2,1)S(1)}, bf16[64,256,128]{2,1,0:T(8,128)(2,1)}, u32[]{:S(2)}) copy-start(bf16[64,256,128]{2,1,0:T(8,128)(2,1)} %fine.1) | copy-start | bytes 12582916
  3.4 0.7 %copy-start.5 = (s32[8,256]{1,0:T(8,128)S(1)}, s32[8,256]{1,0:T(8,128)}, u32[]{:S(2)}) copy-start(s32[8,256]{1,0:T(8,128)} %pattern.1) | copy-start | bytes 24580
  4.1 19.4 %copy-start.2 = (bf16[8,128,128]{2,1,0:T(8,128)(2,1)S(1)}, bf16[8,128,128]{2,1,0:T(8,128)(2,1)}, u32[]{:S(2)}) copy-start(bf16[8,128,128]{2,1,0:T(8,128)(2,1)} %refs_10_.1) | copy-start | bytes 786436
  7.0 1.5 %collective-permute-start = (bf16[5,64,128]{2,1,0:T(8,128)(2,1)S(1)}, bf16[5,64,128]{2,1,0:T(8,128)(2,1)S(1)}, u32[]{:S(2)}, u32[]{:S(2)}) collective-permute-start(bf16[5,64,128]{2,1,0:T(8,128)(2,1)S(1)} %get-tuple-element.22), channel_id=1, source_target_pairs={{0,1},{1,0},{2,3},{3,2},{4,5},{5,4},{6,7},{7,6},{8,9},{9,8},{10,11... | collective-permute-start | bytes 245768 | tf_op jit(solution)/shard_map/ppermute | solution.py:365
  8.5 4.8 %collective-permute-start.1 = (bf16[4,64,128]{2,1,0:T(8,128)(2,1)S(1)}, bf16[4,64,128]{2,1,0:T(8,128)(2,1)S(1)}, u32[]{:S(2)}, u32[]{:S(2)}) collective-permute-start(bf16[4,64,128]{2,1,0:T(8,128)(2,1)S(1)} %fusion), channel_id=1, source_target_pairs={{0,3},{1,2},{2,1},{3,0},{4,7},{5,6},{6,5},{7,4},{8,11},{9,10},{10,... | collective-permute-start | bytes 196616 | tf_op jit(solution)/shard_map/ppermute | solution.py:365
  13.4 3.8 %collective-permute-start.2 = (bf16[3,64,128]{2,1,0:T(8,128)(2,1)S(1)}, bf16[3,64,128]{2,1,0:T(8,128)(2,1)S(1)}, u32[]{:S(2)}, u32[]{:S(2)}) collective-permute-start(bf16[3,64,128]{2,1,0:T(8,128)(2,1)S(1)} %slice.44), channel_id=1, source_target_pairs={{0,5},{1,4},{2,7},{3,6},{4,1},{5,0},{6,3},{7,2},{8,13},{9,12},{10,... | collective-permute-start | bytes 147464 | tf_op jit(solution)/shard_map/ppermute | solution.py:365
  17.2 25.4 %collective-permute-start.3 = (bf16[3,64,128]{2,1,0:T(8,128)(2,1)S(1)}, bf16[3,64,128]{2,1,0:T(8,128)(2,1)S(1)}, u32[]{:S(2)}, u32[]{:S(2)}) collective-permute-start(bf16[3,64,128]{2,1,0:T(8,128)(2,1)S(1)} %fusion.1), channel_id=1, source_target_pairs={{0,9},{1,8},{2,11},{3,10},{4,13},{5,12},{6,15},{7,14},{8,1},{9,0},... | collective-permute-start | bytes 147464 | tf_op jit(solution)/shard_map/ppermute | solution.py:365
  19.3 27.7 %collective-permute-start.5 = (bf16[64,128]{1,0:T(8,128)(2,1)S(1)}, bf16[64,128]{1,0:T(8,128)(2,1)S(1)}, u32[]{:S(2)}, u32[]{:S(2)}) collective-permute-start(bf16[64,128]{1,0:T(8,128)(2,1)S(1)} %get-tuple-element.23), channel_id=1, source_target_pairs={{0,31},{1,2},{2,1},{3,4},{4,3},{5,6},{6,5},{7,8},{8,7},{9,10},{10,... | collective-permute-start | bytes 49160 | tf_op jit(solution)/shard_map/ppermute | solution.py:365
  23.5 2.6 %copy-start.1 = (bf16[8,4,128,128]{3,2,1,0:T(8,128)(2,1)S(1)}, bf16[8,4,128,128]{3,2,1,0:T(8,128)(2,1)}, u32[]{:S(2)}) copy-start(bf16[8,4,128,128]{3,2,1,0:T(8,128)(2,1)} %refs_9_.1) | copy-start | bytes 3145732
  23.5 2.6 %copy-start.4 = (bf16[3,128,128]{2,1,0:T(8,128)(2,1)S(1)}, bf16[3,128,128]{2,1,0:T(8,128)(2,1)}, u32[]{:S(2)}) copy-start(bf16[3,128,128]{2,1,0:T(8,128)(2,1)} %refs_8_.1) | copy-start | bytes 294916
  42.6 4.3 %collective-permute-start.4 = (bf16[2,64,128]{2,1,0:T(8,128)(2,1)S(1)}, bf16[2,64,128]{2,1,0:T(8,128)(2,1)S(1)}, u32[]{:S(2)}, u32[]{:S(2)}) collective-permute-start(bf16[2,64,128]{2,1,0:T(8,128)(2,1)S(1)} %slice.45), channel_id=1, source_target_pairs={{0,17},{1,16},{2,19},{3,18},{4,21},{5,20},{6,23},{7,22},{8,25},{9,... | collective-permute-start | bytes 98312 | tf_op jit(solution)/shard_map/ppermute | solution.py:365

commit v2 on v1

--- a/solution.py
+++ b/solution.py
@@ -7,6 +7,7 @@
 from jax.experimental.pallas import tpu as pltpu
 from jax.sharding import PartitionSpec as P
 
+
 BF = jnp.bfloat16
 F32 = jnp.float32
 MIB = 1 << 20
@@ -25,8 +26,7 @@
 
 
 class Plan:
-    def __init__(self, devices, fine, pattern, restrict):
-        self.devices = devices
+    def __init__(self, devices, fine, restrict):
         self.nv, self.blocks, self.width = fine.shape
         self.levels, self.kinds = restrict.shape[:2]
         total = self.blocks * devices
@@ -59,7 +59,6 @@
             self.col[l] = at
             at += self.kinds * self.runs[l]
         self.cols = -(-at // 128) * 128
-        self.used_cols = at
         self.top_cols = self.kinds * len(self.top)
 
     def target(self, pat, l, base):
@@ -167,8 +166,6 @@
 
 def kernel_b1(plan, g_mid, g_thin, restrict, inverse, lsm):
     nv, kinds, width = plan.nv, plan.kinds, plan.width
-    lv = plan.mid + plan.thin
-    base = lv[0]
     lthin = g_thin
     for l in plan.mid:
         runs = plan.runs[l]
@@ -327,7 +324,7 @@
 
 def shards(fine, pattern, stencil, restrict, coarse_inv):
     devices = lax.axis_size("gx")
-    plan = Plan(devices, fine, pattern, restrict)
+    plan = Plan(devices, fine, restrict)
     nv, blocks, width = fine.shape
     ntop = len(plan.top)
     chunks = 8
@@ -359,7 +356,11 @@
         ],
         compiler_params=params(12),
         name="gather_sums",
-    )(fine, pattern, restrict)
+    )(
+        pltpu.with_memory_space_constraint(fine, pltpu.HBM),
+        pltpu.with_memory_space_constraint(pattern, pltpu.HBM),
+        pltpu.with_memory_space_constraint(restrict, pltpu.HBM),
+    )
 
     def permute(x, to):
         return lax.ppermute(x, "gx", [(i, to(i) % devices) for i in range(devices)])
@@ -380,16 +381,16 @@
     counts = [nv // nparts] * nparts
     parts = []
     for n in range(nparts):
-        parts.append(
-            pl.pallas_call(
-                functools.partial(kernel_b, plan, sum(counts[:n]), counts[n]),
-                out_shape=vm((counts[n], blocks, width), F32),
-                in_specs=[vmem_spec()] * 8,
-                out_specs=vmem_spec(),
-                compiler_params=params(16),
-                name="local_part",
-            )(fine_v, m1, mt1, mt2, lsm, stencil, restrict, coarse_inv)
-        )
+      parts.append(
+          pl.pallas_call(
+              functools.partial(kernel_b, plan, sum(counts[:n]), counts[n]),
+              out_shape=vm((counts[n], blocks, width), F32),
+              in_specs=[vmem_spec()] * 8,
+              out_specs=vmem_spec(),
+              compiler_params=params(16),
+              name="local_part",
+          )(fine_v, m1, mt1, mt2, lsm, stencil, restrict, coarse_inv)
+      )
 
     done = [None] * ntop
     live = tops
@@ -435,4 +436,5 @@
 def solution(mesh):
     in_specs = (P(None, "gx", None), P(None, "gx"), P(), P(), P())
     out_specs = P(None, "gx", None)
+
     return jax.shard_map(shards, mesh=mesh, in_specs=in_specs, out_specs=out_specs, check_vma=False)

time: 52.6 us -> 49.9 us (0.949)
  local copies, waits for them, and re-layouts: 4.15 us -> 0.04 us
  Pallas kernels: 27.3 us -> 28.8 us
    unnamed x12 -> x6, local copies, waits for them, and re-layouts: 4.12 us -> 0.01 us
    pallas_call x1, Pallas kernels: 2.89 us -> 4.47 us  [shards(): pl.pallas_call(functools.partial(kernel_a, plan), out_shape=a_out, in_spe...]
  transfers between devices with their start and end apart: 6 -> 6, of which waited for: 4 -> 4; matrix products, arithmetic and copies ran while one was open for 0% -> 0% of each run, Pallas kernels for 36% -> 38%
where the time goes in v2:
time: 49.9 us; the launch traced here: 49.8 us
  Pallas kernels  28.8 us (58%)
  starting transfers between devices  11.6 us (23%)
  waiting for transfers between devices  9.07 us (18%)
    pallas_call x4, Pallas kernels, shards(): pl.pallas_call(functools.partial(kernel_b, plan, sum(counts[:n]), counts[...  16.3 us
    ppermute x6, starting transfers between devices, permute(): return lax.ppermute(x, 'gx', [(i, to(i) % devices) for i in range(devices)])  11.6 us
    ppermute x6, waiting for transfers between devices, permute(): return lax.ppermute(x, 'gx', [(i, to(i) % devices) for i in range(devices)])  9.07 us
    pallas_call x1, Pallas kernels, shards(): pl.pallas_call(functools.partial(kernel_c, plan, counts), out_shape=jax.S...  5.41 us
    pallas_call x1, Pallas kernels, shards(): pl.pallas_call(functools.partial(kernel_a, plan), out_shape=a_out, in_spe...  4.47 us
    pallas_call x1, Pallas kernels, shards(): pl.pallas_call(functools.partial(kernel_b1, plan), out_shape=vm((nv, plan...  2.57 us
  transfers between devices with their start and end apart: 6, of which 4 were waited for; matrix products, arithmetic and copies ran while one was open for 0% of the time, Pallas kernels for 38%

profile of v2, /device:TPU:0, one launch (start us, length us, event | category | flops | bytes accessed | tf_op | source)
XLA Modules:
  0.0 49.8 jit_solution(16294816950316743993)
XLA Ops:
  0.0 0.0 copy-start
  0.0 0.0 copy-start.1
  0.0 4.5 %gather_sums.1 = (bf16[64,256,128]{2,1,0:T(8,128)(2,1)S(1)}, bf16[4096,128]{1,0:T(8,128)(2,1)S(1)}, f32[2560,128]{1,0:T(8,128)S(1)}, f32[4,64,128]{2,1,0:T(8,128...) custom-call(bf16[64,256,128]{2,1,0:T(8,128)(2,1)} %fine.1, ...), custom_call_target="tpu_custom_call" | custom-call | tf_op jit(solution)/shard_map/gather_sums/pallas_call | solution.py:344
  4.5 0.6 %collective-permute-start = (bf16[5,64,128]{2,1,0:T(8,128)(2,1)S(1)}, bf16[5,64,128]{2,1,0:T(8,128)(2,1)S(1)}, u32[]{:S(2)}, u32[]{:S(2)}) collective-permute-start(bf16[5,64,128]{2,1,0:T(8,128)(2,1)S(1)} %get-tuple-element.22), channel_id=1, source_target_pairs={{0,1},{1,0},{2,3},{3,2},{4,5},{5,4},{6,7},{7,6},{8,9},{9,8},{10,11... | collective-permute-start | bytes 245768 | tf_op jit(solution)/shard_map/ppermute | solution.py:366
  5.0 0.9 %collective-permute-done = bf16[5,64,128]{2,1,0:T(8,128)(2,1)S(1)} collective-permute-done((bf16[5,64,128]{2,1,0:T(8,128)(2,1)S(1)}, bf16[5,64,128]{2,1,0:T(8,128)(2,1)S(1)}, u32[]{:S(2)}, u32[]{:S(2)}) %collective-permute-start) | collective-permute-done | bytes 81952 | tf_op jit(solution)/shard_map/ppermute | solution.py:366
  6.0 2.7 %collective-permute-start.1 = (bf16[4,64,128]{2,1,0:T(8,128)(2,1)S(1)}, bf16[4,64,128]{2,1,0:T(8,128)(2,1)S(1)}, u32[]{:S(2)}, u32[]{:S(2)}) collective-permute-start(bf16[4,64,128]{2,1,0:T(8,128)(2,1)S(1)} %fusion), channel_id=1, source_target_pairs={{0,3},{1,2},{2,1},{3,0},{4,7},{5,6},{6,5},{7,4},{8,11},{9,10},{10,... | collective-permute-start | bytes 196616 | tf_op jit(solution)/shard_map/ppermute | solution.py:366
  8.7 2.2 %collective-permute-done.1 = bf16[4,64,128]{2,1,0:T(8,128)(2,1)S(1)} collective-permute-done((bf16[4,64,128]{2,1,0:T(8,128)(2,1)S(1)}, bf16[4,64,128]{2,1,0:T(8,128)(2,1)S(1)}, u32[]{:S(2)}, u32[]{:S(2)}) %collective-permute-start.1) | collective-permute-done | bytes 65568 | tf_op jit(solution)/shard_map/ppermute | solution.py:366
  10.9 1.9 %collective-permute-start.2 = (bf16[3,64,128]{2,1,0:T(8,128)(2,1)S(1)}, bf16[3,64,128]{2,1,0:T(8,128)(2,1)S(1)}, u32[]{:S(2)}, u32[]{:S(2)}) collective-permute-start(bf16[3,64,128]{2,1,0:T(8,128)(2,1)S(1)} %slice.44), channel_id=1, source_target_pairs={{0,5},{1,4},{2,7},{3,6},{4,1},{5,0},{6,3},{7,2},{8,13},{9,12},{10,... | collective-permute-start | bytes 147464 | tf_op jit(solution)/shard_map/ppermute | solution.py:366
  12.8 1.8 %collective-permute-done.2 = bf16[3,64,128]{2,1,0:T(8,128)(2,1)S(1)} collective-permute-done((bf16[3,64,128]{2,1,0:T(8,128)(2,1)S(1)}, bf16[3,64,128]{2,1,0:T(8,128)(2,1)S(1)}, u32[]{:S(2)}, u32[]{:S(2)}) %collective-permute-start.2) | collective-permute-done | bytes 49184 | tf_op jit(solution)/shard_map/ppermute | solution.py:366
  14.6 2.1 %collective-permute-start.3 = (bf16[3,64,128]{2,1,0:T(8,128)(2,1)S(1)}, bf16[3,64,128]{2,1,0:T(8,128)(2,1)S(1)}, u32[]{:S(2)}, u32[]{:S(2)}) collective-permute-start(bf16[3,64,128]{2,1,0:T(8,128)(2,1)S(1)} %fusion.1), channel_id=1, source_target_pairs={{0,9},{1,8},{2,11},{3,10},{4,13},{5,12},{6,15},{7,14},{8,1},{9,0},... | collective-permute-start | bytes 147464 | tf_op jit(solution)/shard_map/ppermute | solution.py:366
  16.7 4.2 %collective-permute-start.5 = (bf16[64,128]{1,0:T(8,128)(2,1)S(1)}, bf16[64,128]{1,0:T(8,128)(2,1)S(1)}, u32[]{:S(2)}, u32[]{:S(2)}) collective-permute-start(bf16[64,128]{1,0:T(8,128)(2,1)S(1)} %get-tuple-element.23), channel_id=1, source_target_pairs={{0,31},{1,2},{2,1},{3,4},{4,3},{5,6},{6,5},{7,8},{8,7},{9,10},{10,... | collective-permute-start | bytes 49160 | tf_op jit(solution)/shard_map/ppermute | solution.py:366
  21.0 0.0 copy-done
  21.0 0.0 copy-done.1
  21.0 2.6 %local_levels.1.lsm = bf16[64,128,128]{2,1,0:T(8,128)(2,1)S(1)} custom-call(bf16[4096,128]{1,0:T(8,128)(2,1)S(1)} %get-tuple-element.19.g_mid, f32[2560,128]{1,0:T(8,128)S(1)} %get-tuple-element.20.g_thin, bf16[8,4,128,128]{3,2,1,0:T(8,128)(2,1)S(1)} %copy-done, bf16[8,128,128]{2,1,0:T(8,128)(2,1)S(1)} %copy-done.1), custom_call_target="tpu_custom_call" | custom-call | tf_op jit(solution)/shard_map/local_levels/pallas_call | solution.py:371
  23.6 0.0 copy-done.2
  23.6 4.1 %local_part.7.refs_3_ = f32[16,256,128]{2,1,0:T(8,128)S(1)} custom-call(bf16[64,256,128]{2,1,0:T(8,128)(2,1)S(1)} %get-tuple-element.15.fine_v, bf16[256,256]{1,0:T(8,128)(2,1)S(1)} %get-tuple-element.16.m1, bf16[256,256]{1,0:T(8,128)(2,1)S(1)} %get-tuple-element.17.mt1, bf16[256,128]{1,0:T(8,128)(2,1)S(1)} %get-tuple-element.18.mt2, ...), custom_call_target="tpu_custom_call" | custom-call | tf_op jit(solution)/shard_map/local_part/pallas_call | solution.py:385
  27.7 4.1 %local_part.6.refs_2_ = f32[16,256,128]{2,1,0:T(8,128)S(1)} custom-call(bf16[64,256,128]{2,1,0:T(8,128)(2,1)S(1)} %get-tuple-element.15.fine_v, bf16[256,256]{1,0:T(8,128)(2,1)S(1)} %get-tuple-element.16.m1, bf16[256,256]{1,0:T(8,128)(2,1)S(1)} %get-tuple-element.17.mt1, bf16[256,128]{1,0:T(8,128)(2,1)S(1)} %get-tuple-element.18.mt2, ...), custom_call_target="tpu_custom_call" | custom-call | tf_op jit(solution)/shard_map/local_part/pallas_call | solution.py:385
  31.8 4.1 %local_part.5.refs_1_ = f32[16,256,128]{2,1,0:T(8,128)S(1)} custom-call(bf16[64,256,128]{2,1,0:T(8,128)(2,1)S(1)} %get-tuple-element.15.fine_v, bf16[256,256]{1,0:T(8,128)(2,1)S(1)} %get-tuple-element.16.m1, bf16[256,256]{1,0:T(8,128)(2,1)S(1)} %get-tuple-element.17.mt1, bf16[256,128]{1,0:T(8,128)(2,1)S(1)} %get-tuple-element.18.mt2, ...), custom_call_target="tpu_custom_call" | custom-call | tf_op jit(solution)/shard_map/local_part/pallas_call | solution.py:385
  35.9 4.1 %local_part.4.refs_0_ = f32[16,256,128]{2,1,0:T(8,128)S(1)} custom-call(bf16[64,256,128]{2,1,0:T(8,128)(2,1)S(1)} %get-tuple-element.15.fine_v, bf16[256,256]{1,0:T(8,128)(2,1)S(1)} %get-tuple-element.16.m1, bf16[256,256]{1,0:T(8,128)(2,1)S(1)} %get-tuple-element.17.mt1, bf16[256,128]{1,0:T(8,128)(2,1)S(1)} %get-tuple-element.18.mt2, ...), custom_call_target="tpu_custom_call" | custom-call | tf_op jit(solution)/shard_map/local_part/pallas_call | solution.py:385
  40.0 0.0 collective-permute-done.3
  40.0 0.1 collective-permute-start.4
  40.1 4.2 %collective-permute-done.4 = bf16[2,64,128]{2,1,0:T(8,128)(2,1)S(1)} collective-permute-done((bf16[2,64,128]{2,1,0:T(8,128)(2,1)S(1)}, bf16[2,64,128]{2,1,0:T(8,128)(2,1)S(1)}, u32[]{:S(2)}, u32[]{:S(2)}) %collective-permute-start.4) | collective-permute-done | bytes 32800 | tf_op jit(solution)/shard_map/ppermute | solution.py:366
  44.3 0.0 collective-permute-done.5.refs_6_
  44.3 5.4 %finish.1 = f32[64,256,128]{2,1,0:T(8,128)} custom-call(f32[16,256,128]{2,1,0:T(8,128)S(1)} %local_part.4.refs_0_, f32[16,256,128]{2,1,0:T(8,128)S(1)} %local_part.5.refs_1_, f32[16,256,128]{2,1,0:T(8,128)S(1)} %local_part.6.refs_2_, f32[16,256,128]{2,1,0:T(8,128)S(1)} %local_part.7.refs_3_, f32[4,64,128]{2,1,0:T(8,128)S(1)} %pad_maximum_fusion.refs_4_, ...), custom_call_target="tpu_custom_call" | custom-call | tf_op jit(solution)/shard_map/finish/pallas_call | solution.py:419
  (12 shorter events, 0.1 us)
Async XLA Ops:
  0.0 21.0 %copy-start = (bf16[8,4,128,128]{3,2,1,0:T(8,128)(2,1)S(1)}, bf16[8,4,128,128]{3,2,1,0:T(8,128)(2,1)}, u32[]{:S(2)}) copy-start(bf16[8,4,128,128]{3,2,1,0:T(8,128)(2,1)} %refs_9_.1) | copy-start | bytes 3145732
  0.0 21.0 %copy-start.1 = (bf16[8,128,128]{2,1,0:T(8,128)(2,1)S(1)}, bf16[8,128,128]{2,1,0:T(8,128)(2,1)}, u32[]{:S(2)}) copy-start(bf16[8,128,128]{2,1,0:T(8,128)(2,1)} %refs_10_.1) | copy-start | bytes 786436
  4.5 1.5 %collective-permute-start = (bf16[5,64,128]{2,1,0:T(8,128)(2,1)S(1)}, bf16[5,64,128]{2,1,0:T(8,128)(2,1)S(1)}, u32[]{:S(2)}, u32[]{:S(2)}) collective-permute-start(bf16[5,64,128]{2,1,0:T(8,128)(2,1)S(1)} %get-tuple-element.22), channel_id=1, source_target_pairs={{0,1},{1,0},{2,3},{3,2},{4,5},{5,4},{6,7},{7,6},{8,9},{9,8},{10,11... | collective-permute-start | bytes 245768 | tf_op jit(solution)/shard_map/ppermute | solution.py:366
  6.0 4.9 %collective-permute-start.1 = (bf16[4,64,128]{2,1,0:T(8,128)(2,1)S(1)}, bf16[4,64,128]{2,1,0:T(8,128)(2,1)S(1)}, u32[]{:S(2)}, u32[]{:S(2)}) collective-permute-start(bf16[4,64,128]{2,1,0:T(8,128)(2,1)S(1)} %fusion), channel_id=1, source_target_pairs={{0,3},{1,2},{2,1},{3,0},{4,7},{5,6},{6,5},{7,4},{8,11},{9,10},{10,... | collective-permute-start | bytes 196616 | tf_op jit(solution)/shard_map/ppermute | solution.py:366
  10.9 3.7 %collective-permute-start.2 = (bf16[3,64,128]{2,1,0:T(8,128)(2,1)S(1)}, bf16[3,64,128]{2,1,0:T(8,128)(2,1)S(1)}, u32[]{:S(2)}, u32[]{:S(2)}) collective-permute-start(bf16[3,64,128]{2,1,0:T(8,128)(2,1)S(1)} %slice.44), channel_id=1, source_target_pairs={{0,5},{1,4},{2,7},{3,6},{4,1},{5,0},{6,3},{7,2},{8,13},{9,12},{10,... | collective-permute-start | bytes 147464 | tf_op jit(solution)/shard_map/ppermute | solution.py:366
  14.6 25.3 %collective-permute-start.3 = (bf16[3,64,128]{2,1,0:T(8,128)(2,1)S(1)}, bf16[3,64,128]{2,1,0:T(8,128)(2,1)S(1)}, u32[]{:S(2)}, u32[]{:S(2)}) collective-permute-start(bf16[3,64,128]{2,1,0:T(8,128)(2,1)S(1)} %fusion.1), channel_id=1, source_target_pairs={{0,9},{1,8},{2,11},{3,10},{4,13},{5,12},{6,15},{7,14},{8,1},{9,0},... | collective-permute-start | bytes 147464 | tf_op jit(solution)/shard_map/ppermute | solution.py:366
  16.7 27.6 %collective-permute-start.5 = (bf16[64,128]{1,0:T(8,128)(2,1)S(1)}, bf16[64,128]{1,0:T(8,128)(2,1)S(1)}, u32[]{:S(2)}, u32[]{:S(2)}) collective-permute-start(bf16[64,128]{1,0:T(8,128)(2,1)S(1)} %get-tuple-element.23), channel_id=1, source_target_pairs={{0,31},{1,2},{2,1},{3,4},{4,3},{5,6},{6,5},{7,8},{8,7},{9,10},{10,... | collective-permute-start | bytes 49160 | tf_op jit(solution)/shard_map/ppermute | solution.py:366
  21.0 2.6 %copy-start.2 = (bf16[3,128,128]{2,1,0:T(8,128)(2,1)S(1)}, bf16[3,128,128]{2,1,0:T(8,128)(2,1)}, u32[]{:S(2)}) copy-start(bf16[3,128,128]{2,1,0:T(8,128)(2,1)} %refs_8_.1) | copy-start | bytes 294916
  40.0 4.3 %collective-permute-start.4 = (bf16[2,64,128]{2,1,0:T(8,128)(2,1)S(1)}, bf16[2,64,128]{2,1,0:T(8,128)(2,1)S(1)}, u32[]{:S(2)}, u32[]{:S(2)}) collective-permute-start(bf16[2,64,128]{2,1,0:T(8,128)(2,1)S(1)} %slice.45), channel_id=1, source_target_pairs={{0,17},{1,16},{2,19},{3,18},{4,21},{5,20},{6,23},{7,22},{8,25},{9,... | collective-permute-start | bytes 98312 | tf_op jit(solution)/shard_map/ppermute | solution.py:366

commit v3 on v1

v3 whole, which is shorter than its diff:
```python
import functools

import jax
import jax.numpy as jnp
from jax import lax
from jax.experimental import pallas as pl
from jax.experimental.pallas import tpu as pltpu
from jax.sharding import PartitionSpec as P


BF = jnp.bfloat16
F32 = jnp.float32
MIB = 1 << 20
PARTS = (4, 4, 4, 4)
CHUNKS = (6, 4, 4, 2)
GROUP = 8


def dot(a, b):
    return jnp.dot(a, b, preferred_element_type=F32)


def vmem_spec():
    return pl.BlockSpec(memory_space=pltpu.VMEM)


def any_spec():
    return pl.BlockSpec(memory_space=pltpu.HBM)


class Plan:
    def __init__(self, devices, fine, restrict):
        self.nv, self.blocks, self.width = fine.shape
        self.levels, self.kinds = restrict.shape[:2]
        total = self.blocks * devices
        self.spans = []
        for level in range(self.levels):
            self.spans.append(total // max(total // 4 ** (level + 1), 1))
        self.runs = [self.blocks // min(s, self.blocks) for s in self.spans]
        local = [l for l in range(self.levels) if self.spans[l] <= self.blocks]
        self.top = [l for l in range(self.levels) if self.spans[l] > self.blocks]
        self.wide = [l for l in local if self.runs[l] * self.kinds == self.blocks]
        self.mid = [l for l in local if l not in self.wide and self.runs[l] % 16 == 0]
        self.thin = [l for l in local if l not in self.wide and l not in self.mid]
        self.row = {}
        at = 0
        for l in self.mid:
            self.row[l] = at
            at += self.kinds * self.runs[l]
        self.mid_rows = at
        at = 0
        for l in self.thin + self.top:
            self.row[l] = at
            at += self.kinds * self.runs[l]
        self.first_row = at
        self.last_row = at + 1
        self.thin_rows = -(-(at + 2) // 8) * 8
        self.a_rows = -(-(self.mid_rows + self.thin_rows) // 16) * 16
        self.col = {}
        at = 0
        for l in self.mid + self.thin:
            self.col[l] = at
            at += self.kinds * self.runs[l]
        self.cols = -(-at // 128) * 128
        self.used_cols = at
        self.top_cols = self.kinds * len(self.top)

    def target(self, pat, l, base):
        index = lax.broadcasted_iota(jnp.int32, (1, self.blocks), 1)
        run = index // min(self.spans[l], self.blocks)
        return base + pat[l : l + 1, :] * self.runs[l] + run


def onehot(hit):
    return jnp.where(hit, 1.0, 0.0)


def kernel_a(plan, fine, pattern, restrict, inverse, stencil, fine_v, g_mid, g_thin, tops, msg, hb, m1, mt1, mt2, mtop, r_v, inv_v, sten_v, pat_s, m_s, sems, psem, wsem):
    nv, blocks, width = plan.nv, plan.blocks, plan.width
    kinds = plan.kinds
    ntop = len(plan.top)
    sizes = [nv * c // sum(CHUNKS) for c in CHUNKS]
    chunks = len(sizes)

    def chunk_copy(n):
        at = pl.ds(sum(sizes[:n]), sizes[n])
        return pltpu.make_async_copy(fine.at[at], fine_v.at[at], sems.at[n])

    pcopy = pltpu.make_async_copy(pattern, pat_s, psem)
    pcopy.start()
    for n in range(chunks):
        chunk_copy(n).start()
    at = pl.ds(plan.top[0], ntop)
    below = pl.ds(0, plan.top[0])
    weights = [
        pltpu.make_async_copy(restrict.at[at], r_v.at[at], wsem.at[0]),
        pltpu.make_async_copy(restrict.at[below], r_v.at[below], wsem.at[1]),
        pltpu.make_async_copy(inverse, inv_v, wsem.at[2]),
        pltpu.make_async_copy(stencil, sten_v, wsem.at[3]),
    ]
    for w in weights:
        w.start()
    pcopy.wait()
    pat = pat_s[...]
    rows = lax.broadcasted_iota(jnp.int32, (plan.mid_rows, blocks), 0)
    hit = rows == plan.target(pat, plan.mid[0], plan.row[plan.mid[0]])
    for l in plan.mid[1:]:
        hit = hit | (rows == plan.target(pat, l, plan.row[l]))
    m_s[pl.ds(0, plan.mid_rows), :] = onehot(hit).astype(BF)
    rest = plan.a_rows - plan.mid_rows
    rows = lax.broadcasted_iota(jnp.int32, (rest, blocks), 0)
    cols = lax.broadcasted_iota(jnp.int32, (rest, blocks), 1)
    hit = ((rows == plan.first_row) & (cols == 0)) | ((rows == plan.last_row) & (cols == blocks - 1))
    for l in plan.thin + plan.top:
        hit = hit | (rows == plan.target(pat, l, plan.row[l]))
    m_s[pl.ds(plan.mid_rows, rest), :] = onehot(hit).astype(BF)

    t_wide = plan.target(pat, plan.wide[0], 0)
    wrows = lax.broadcasted_iota(jnp.int32, (blocks, blocks), 0)
    m1[...] = onehot(wrows == t_wide).astype(BF)
    lane = lax.broadcasted_iota(jnp.int32, (blocks, 128), 1).astype(F32)
    tw = jnp.broadcast_to(t_wide.astype(F32), (128, blocks)).T
    for n in range(blocks // 128):
        mt1[:, pl.ds(n * 128, 128)] = onehot(tw == lane + float(n * 128)).astype(BF)
    rows = lax.broadcasted_iota(jnp.int32, (plan.cols, blocks), 0)
    hit = jnp.zeros(rows.shape, jnp.bool_)
    for l in plan.mid + plan.thin:
        hit = hit | (rows == plan.target(pat, l, plan.col[l]))
    mt2[...] = onehot(hit).T.astype(BF)
    rows = lax.broadcasted_iota(jnp.int32, (128, blocks), 0)
    hit = jnp.zeros(rows.shape, jnp.bool_)
    for n, l in enumerate(plan.top):
        hit = hit | (rows == pat[l : l + 1, :] + n * kinds)
    mtop[...] = onehot(hit).T.astype(BF)
    m = m_s[...]
    for n in range(chunks):
        chunk_copy(n).wait()
        for p in range(sizes[n] // 2):
            v = sum(sizes[:n]) + 2 * p
            pair = jnp.concatenate([fine_v[v], fine_v[v + 1]], axis=1)
            g = dot(m, pair)
            for h in range(2):
                half = g[:, h * width : (h + 1) * width]
                for l in plan.mid:
                    runs = plan.runs[l]
                    for k in range(kinds):
                        r = plan.row[l] + k * runs
                        o = plan.row[l] * nv + k * runs * nv
                        g_mid[pl.ds(o + (v + h) * runs, runs), :] = half[r : r + runs].astype(BF)
                g_thin[pl.ds((v + h) * plan.thin_rows, plan.thin_rows), :] = half[
                    plan.mid_rows : plan.mid_rows + plan.thin_rows
                ]
    weights[0].wait()
    for n, l in enumerate(plan.top):
        parts = [
            g_thin[pl.ds(plan.row[l] + k, nv, stride=plan.thin_rows), :].astype(BF) for k in range(kinds)
        ]
        tile = flat(r_v, l, kinds)
        coarse = dot(jnp.concatenate(parts, axis=1), tile)
        tops[n] = coarse
        msg[n] = coarse.astype(BF)
    first = g_thin[pl.ds(plan.first_row, nv, stride=plan.thin_rows), :].astype(BF)
    last = g_thin[pl.ds(plan.last_row, nv, stride=plan.thin_rows), :].astype(BF)
    odd = lax.axis_index("gx") % 2 == 1
    msg[ntop] = jnp.where(odd, first, last)
    hb[...] = jnp.where(odd, last, first)

    for w in weights[1:]:
        w.wait()


def flat(restrict, l, kinds):
    return jnp.concatenate([restrict[l, k] for k in range(kinds)], axis=0)


def flat_t(restrict, l, kinds):
    return jnp.concatenate([restrict[l, k].T for k in range(kinds)], axis=1)


def chain(plan, l, parts, tiles, inverse, tiles_t):
    coarse = dot(jnp.concatenate(parts, axis=1), tiles) * plan.spans[l] ** (-0.5)
    solved = dot(coarse.astype(BF), inverse).astype(BF)
    return dot(solved, tiles_t)


def kernel_b1(plan, g_mid, g_thin, restrict, inverse, lsm, t_wide, rt_top, scr):
    nv, kinds, width = plan.nv, plan.kinds, plan.width
    l = plan.wide[0]
    w = dot(flat(restrict, l, kinds), inverse[l]) * plan.spans[l] ** (-0.5)
    high = w.astype(BF)
    low = (w - high.astype(F32)).astype(BF)
    tiles_t = flat_t(restrict, l, kinds)
    t_wide[...] = (dot(high, tiles_t) + dot(low, tiles_t)).astype(BF)
    for n, l in enumerate(plan.top):
        rt_top[n] = flat_t(restrict, l, kinds)
    for l in plan.mid:
        runs = plan.runs[l]
        o = plan.row[l] * nv
        tiles = flat(restrict, l, kinds)
        tiles_t = flat_t(restrict, l, kinds)
        step = min(nv, 16)

        def mid_step(n, carry, l=l, runs=runs, o=o, tiles=tiles, tiles_t=tiles_t):
            parts = [
                g_mid[pl.ds(o + k * nv * runs + n * (step * runs), step * runs), :]
                for k in range(kinds)
            ]
            lifted = chain(plan, l, parts, tiles, inverse[l], tiles_t).astype(BF)
            for v in range(step):
                for k in range(kinds):
                    lsm[n * step + v, pl.ds(plan.col[l] + k * runs, runs), :] = lifted[
                        v * runs : (v + 1) * runs, k * width : (k + 1) * width
                    ]
            return carry

        for n in range(nv // step):
            mid_step(n, 0)
    rows_at = plan.col[plan.thin[0]]
    thin_cols = plan.used_cols - rows_at
    padded = -(-thin_cols // 8) * 8
    for l in plan.thin:
        runs = plan.runs[l]
        parts = []
        for k in range(kinds):
            rows = [
                g_thin[pl.ds(plan.row[l] + k * runs + j, nv, stride=plan.thin_rows), :].astype(BF)
                for j in range(runs)
            ]
            parts.append(jnp.concatenate(rows, axis=0))
        lifted = chain(plan, l, parts, flat(restrict, l, kinds), inverse[l], flat_t(restrict, l, kinds))
        for j in range(runs):
            for k in range(kinds):
                at = plan.col[l] - rows_at + k * runs + j
                scr[pl.ds(at * nv, nv), :] = lifted[j * nv : (j + 1) * nv, k * width : (k + 1) * width]
    for at in range(thin_cols, padded):
        scr[pl.ds(at * nv, nv), :] = jnp.zeros((nv, width), F32)
    pad = jnp.zeros((plan.cols - rows_at - padded, width), F32)

    def spread(n, carry):
        for q in range(8):
            v = n * 8 + q
            rows = scr[pl.ds(v, padded, stride=nv), :]
            lsm[v, pl.ds(rows_at, plan.cols - rows_at), :] = jnp.concatenate([rows, pad], axis=0).astype(BF)
        return carry

    for n in range(nv // 8):
        spread(n, 0)


def kernel_b(plan, start, count, fine_v, m1, mt1, mt2, lsm, stencil, t_wide, *refs):
    out, scr_s = refs[-2:]
    kinds, width, blocks = plan.kinds, plan.width, plan.blocks
    l = plan.wide[0]
    runs = plan.runs[l]
    group = GROUP
    scr_s[:width, :width] = stencil[1]
    scr_s[:width, width:] = stencil[0]
    scr_s[width:, :width] = stencil[2]
    scr_s[width:, width:] = jnp.zeros((width, width), BF)
    rowid = lax.broadcasted_iota(jnp.int32, (blocks, width), 0)

    def step(n, carry):
        v0 = start + n * group
        fs = [fine_v[v0 + q] for q in range(group)]
        gs = []
        for p in range(group // 2):
            pair = jnp.concatenate([fs[2 * p], fs[2 * p + 1]], axis=1)
            g = dot(m1[...], pair).astype(BF)
            gs.append(g[:, :width])
            gs.append(g[:, width:])
        parts = [
            jnp.concatenate([g[k * runs : (k + 1) * runs] for g in gs], axis=0) for k in range(kinds)
        ]
        lifted = dot(jnp.concatenate(parts, axis=1), t_wide[...]).astype(BF)
        for p in range(group // 2):
            halves = []
            for q in (2 * p, 2 * p + 1):
                rows = [
                    lifted[q * runs : (q + 1) * runs, k * width : (k + 1) * width] for k in range(kinds)
                ]
                halves.append(jnp.concatenate(rows + [lsm[v0 + q]], axis=0))
            big = jnp.concatenate(halves, axis=1)
            e = dot(mt1[...], big[:blocks]) + dot(mt2[...], big[blocks:])
            for h in range(2):
                q = 2 * p + h
                f = fs[q].astype(F32)
                nxt = jnp.where(rowid == blocks - 1, 0.0, pltpu.roll(f, blocks - 1, 0)).astype(BF)
                y = dot(jnp.concatenate([fs[q], nxt], axis=1), scr_s[...])
                prev = jnp.where(rowid == 0, 0.0, pltpu.roll(y[:, width:], 1, 0))
                out[v0 + q] = e[:, h * width : (h + 1) * width] + y[:, :width] + prev
        return carry

    lax.fori_loop(0, count // group, step, 0)


def kernel_c(plan, res, sums, halo_r, halo_o, mtop, stencil, rt_top, inverse, out, lt, h0, h2, ring, sems):
    nv, kinds, width, blocks = plan.nv, plan.kinds, plan.width, plan.blocks
    tcols = plan.top_cols
    for n, l in enumerate(plan.top):
        coarse = (sums[n] * plan.spans[l] ** (-0.5)).astype(BF)
        solved = dot(coarse, inverse[l]).astype(BF)
        lifted = dot(solved, rt_top[n])
        for k in range(kinds):
            lt[pl.ds((n * kinds + k) * nv, nv), :] = lifted[:, k * width : (k + 1) * width]
    odd = lax.axis_index("gx") % 2 == 1
    hr = halo_r[...]
    ho = halo_o[...]
    h0[...] = dot(jnp.where(odd, hr, ho), stencil[0])
    h2[...] = dot(jnp.where(odd, ho, hr), stencil[2])
    steps, per = ring.shape[:2]

    def copy(n):
        return pltpu.make_async_copy(ring.at[n], out.at[pl.ds(n * per, per)], sems.at[n])

    mt = mtop[...][:, :tcols]
    for n in range(steps):
        for p in range(per // 2):
            v = n * per + 2 * p
            pair = jnp.concatenate(
                [lt[pl.ds(v, tcols, stride=nv), :], lt[pl.ds(v + 1, tcols, stride=nv), :]], axis=1
            ).astype(BF)
            e = dot(mt, pair)
            for h in range(2):
                ring[n, 2 * p + h] = res[v + h] + e[:, h * width : (h + 1) * width]
                ring[n, 2 * p + h, pl.ds(0, 1), :] += h0[pl.ds(v + h, 1), :]
                ring[n, 2 * p + h, pl.ds(blocks - 1, 1), :] += h2[pl.ds(v + h, 1), :]
        copy(n).start()
    for n in range(steps):
        copy(n).wait()


def params(mib):
    return pltpu.CompilerParams(vmem_limit_bytes=mib * MIB)


def shards(fine, pattern, stencil, restrict, coarse_inv):
    devices = lax.axis_size("gx")
    plan = Plan(devices, fine, restrict)
    nv, blocks, width = fine.shape
    ntop = len(plan.top)
    chunks = len(CHUNKS)
    vm = pltpu.VMEM
    a_out = (
        vm(fine.shape, BF),
        vm((plan.mid_rows * nv, width), BF),
        vm((plan.thin_rows * nv, width), F32),
        vm((ntop, nv, width), F32),
        vm((ntop + 1, nv, width), BF),
        vm((nv, width), BF),
        vm((blocks, blocks), BF),
        vm((blocks, blocks), BF),
        vm((blocks, 128), BF),
        vm((blocks, 128), BF),
        vm(restrict.shape, BF),
        vm(coarse_inv.shape, BF),
        vm(stencil.shape, BF),
    )
    fine_v, g_mid, g_thin, tops, msg, hb, m1, mt1, mt2, mtop, r_v, inv_v, sten_v = pl.pallas_call(
        functools.partial(kernel_a, plan),
        out_shape=a_out,
        in_specs=[any_spec()] * 5,
        out_specs=tuple(vmem_spec() for _ in a_out),
        scratch_shapes=[
            pltpu.VMEM(pattern.shape, jnp.int32),
            pltpu.VMEM((plan.a_rows, blocks), BF),
            pltpu.SemaphoreType.DMA((chunks,)),
            pltpu.SemaphoreType.DMA,
            pltpu.SemaphoreType.DMA((4,)),
        ],
        compiler_params=params(12),
        name="gather_sums",
    )(*(pltpu.with_memory_space_constraint(x, pltpu.HBM) for x in (fine, pattern, restrict, coarse_inv, stencil)))

    def permute(x, to):
        return lax.ppermute(x, "gx", [(i, to(i) % devices) for i in range(devices)])

    rounds = devices.bit_length() - 1
    halo_o = permute(hb, lambda i: i + 1 if i % 2 else i - 1)

    lsm, t_wide, rt_top = pl.pallas_call(
        functools.partial(kernel_b1, plan),
        out_shape=(
            vm((nv, plan.cols, width), BF),
            vm((plan.kinds * width, plan.kinds * width), BF),
            vm((ntop, width, plan.kinds * width), BF),
        ),
        in_specs=[vmem_spec()] * 4,
        out_specs=(vmem_spec(),) * 3,
        scratch_shapes=[pltpu.VMEM((32 * nv, width), F32)],
        compiler_params=params(16),
        name="local_levels",
    )(g_mid, g_thin, r_v, inv_v)

    weights = PARTS
    counts = [nv * w // sum(weights) for w in weights]
    result = ()
    for n in range(len(counts)):
        result = (
            pl.pallas_call(
                functools.partial(kernel_b, plan, sum(counts[:n]), counts[n]),
                out_shape=vm((nv, blocks, width), F32),
                in_specs=[vmem_spec()] * (7 + len(result)),
                out_specs=vmem_spec(),
                scratch_shapes=[pltpu.VMEM((2 * width, 2 * width), BF)],
                input_output_aliases={7: 0} if result else {},
                compiler_params=params(12),
                name="local_part",
            )(fine_v, m1, mt1, mt2, lsm, sten_v, t_wide, *result),
        )

    done = [None] * ntop
    live = tops
    alive = list(range(ntop))
    message = msg
    halo_r = None
    for b in range(rounds):
        flip = (1 << b) | 1
        got = permute(message, lambda i: i ^ flip)
        if b == 0:
            halo_r = got[ntop]
            got = got[:ntop]
        live = live + got.astype(F32)
        keep = [p for p in range(len(alive)) if plan.spans[plan.top[alive[p]]] // blocks > 2 << b]
        for p in range(len(alive)):
            if p not in keep:
                done[alive[p]] = live[p]
        if keep and len(keep) < len(alive):
            live = live[keep[0] :]
        alive = [alive[p] for p in keep]
        message = live.astype(BF)
    sums = jnp.stack(done)

    per = 4
    slots = nv // per
    return pl.pallas_call(
        functools.partial(kernel_c, plan),
        out_shape=jax.ShapeDtypeStruct(fine.shape, F32),
        in_specs=[vmem_spec()] * 8,
        out_specs=any_spec(),
        scratch_shapes=[
            pltpu.VMEM((plan.top_cols * nv, width), F32),
            pltpu.VMEM((nv, width), F32),
            pltpu.VMEM((nv, width), F32),
            pltpu.VMEM((slots, per, blocks, width), F32),
            pltpu.SemaphoreType.DMA((slots,)),
        ],
        compiler_params=params(24),
        name="finish",
    )(*result, sums, halo_r, halo_o, mtop, sten_v, rt_top, inv_v)


def solution(mesh):
    in_specs = (P(None, "gx", None), P(None, "gx"), P(), P(), P())
    out_specs = P(None, "gx", None)

    return jax.shard_map(shards, mesh=mesh, in_specs=in_specs, out_specs=out_specs, check_vma=False)
```

time: 52.6 us -> 41.6 us (0.79)
  Pallas kernels: 27.3 us -> 20.5 us
  local copies, waits for them, and re-layouts: 4.15 us -> 0.03 us
    pallas_call x4, Pallas kernels: 16.4 us -> 9.09 us  [shards(): pl.pallas_call(functools.partial(kernel_b, plan, sum(counts[:n]), counts[...]
    unnamed x12 -> x0, local copies, waits for them, and re-layouts: 4.12 us -> none
    pallas_call x1, Pallas kernels: 2.89 us -> 4.04 us  [shards(): pl.pallas_call(functools.partial(kernel_a, plan), out_shape=a_out, in_spe...]
    pallas_call x2, Pallas kernels: 7.97 us -> 7.36 us  [the longest x1 4.33 us: shards(): pl.pallas_call(functools.partial(kernel_c, plan), out_shape=jax.ShapeDtyp...]
  transfers between devices with their start and end apart: 6 -> 6, of which waited for: 4 -> 4; matrix products, arithmetic and copies ran while one was open for 0% -> 0% of each run, Pallas kernels for 36% -> 29%
where the time goes in v3:
time: 41.6 us; the launch traced here: 41.4 us
  Pallas kernels  20.5 us (49%)
  starting transfers between devices  11.6 us (28%)
  waiting for transfers between devices  9.07 us (22%)
    ppermute x6, starting transfers between devices, permute(): return lax.ppermute(x, 'gx', [(i, to(i) % devices) for i in range(devices)])  11.6 us
    pallas_call x4, Pallas kernels, shards(): pl.pallas_call(functools.partial(kernel_b, plan, sum(counts[:n]), counts[...  9.09 us
    ppermute x6, waiting for transfers between devices, permute(): return lax.ppermute(x, 'gx', [(i, to(i) % devices) for i in range(devices)])  9.07 us
    pallas_call x1, Pallas kernels, shards(): pl.pallas_call(functools.partial(kernel_c, plan), out_shape=jax.ShapeDtyp...  4.33 us
    pallas_call x1, Pallas kernels, shards(): pl.pallas_call(functools.partial(kernel_a, plan), out_shape=a_out, in_spe...  4.04 us
    pallas_call x1, Pallas kernels, shards(): pl.pallas_call(functools.partial(kernel_b1, plan), out_shape=(vm((nv, pla...  3.03 us
  transfers between devices with their start and end apart: 6, of which 4 were waited for; matrix products, arithmetic and copies ran while one was open for 0% of the time, Pallas kernels for 29%

profile of v3, /device:TPU:0, one launch (start us, length us, event | category | flops | bytes accessed | tf_op | source)
XLA Modules:
  0.0 41.4 jit_solution(6539170347108102651)
XLA Ops:
  0.0 4.0 %gather_sums.1 = (bf16[64,256,128]{2,1,0:T(8,128)(2,1)S(1)}, bf16[4096,128]{1,0:T(8,128)(2,1)S(1)}, f32[2560,128]{1,0:T(8,128)S(1)}, f32[4,64,128]{2,1,0:T(8,128...) custom-call(bf16[64,256,128]{2,1,0:T(8,128)(2,1)} %fine.1, ...), custom_call_target="tpu_custom_call" | custom-call | tf_op jit(solution)/shard_map/gather_sums/pallas_call | solution.py:358
  4.1 0.6 %collective-permute-start = (bf16[5,64,128]{2,1,0:T(8,128)(2,1)S(1)}, bf16[5,64,128]{2,1,0:T(8,128)(2,1)S(1)}, u32[]{:S(2)}, u32[]{:S(2)}) collective-permute-start(bf16[5,64,128]{2,1,0:T(8,128)(2,1)S(1)} %get-tuple-element.33), channel_id=1, source_target_pairs={{0,1},{1,0},{2,3},{3,2},{4,5},{5,4},{6,7},{7,6},{8,9},{9,8},{10,11... | collective-permute-start | bytes 245768 | tf_op jit(solution)/shard_map/ppermute | solution.py:375
  4.6 0.9 %collective-permute-done = bf16[5,64,128]{2,1,0:T(8,128)(2,1)S(1)} collective-permute-done((bf16[5,64,128]{2,1,0:T(8,128)(2,1)S(1)}, bf16[5,64,128]{2,1,0:T(8,128)(2,1)S(1)}, u32[]{:S(2)}, u32[]{:S(2)}) %collective-permute-start) | collective-permute-done | bytes 81952 | tf_op jit(solution)/shard_map/ppermute | solution.py:375
  5.6 2.7 %collective-permute-start.1 = (bf16[4,64,128]{2,1,0:T(8,128)(2,1)S(1)}, bf16[4,64,128]{2,1,0:T(8,128)(2,1)S(1)}, u32[]{:S(2)}, u32[]{:S(2)}) collective-permute-start(bf16[4,64,128]{2,1,0:T(8,128)(2,1)S(1)} %fusion), channel_id=1, source_target_pairs={{0,3},{1,2},{2,1},{3,0},{4,7},{5,6},{6,5},{7,4},{8,11},{9,10},{10,... | collective-permute-start | bytes 196616 | tf_op jit(solution)/shard_map/ppermute | solution.py:375
  8.2 2.2 %collective-permute-done.1 = bf16[4,64,128]{2,1,0:T(8,128)(2,1)S(1)} collective-permute-done((bf16[4,64,128]{2,1,0:T(8,128)(2,1)S(1)}, bf16[4,64,128]{2,1,0:T(8,128)(2,1)S(1)}, u32[]{:S(2)}, u32[]{:S(2)}) %collective-permute-start.1) | collective-permute-done | bytes 65568 | tf_op jit(solution)/shard_map/ppermute | solution.py:375
  10.4 2.0 %collective-permute-start.2 = (bf16[3,64,128]{2,1,0:T(8,128)(2,1)S(1)}, bf16[3,64,128]{2,1,0:T(8,128)(2,1)S(1)}, u32[]{:S(2)}, u32[]{:S(2)}) collective-permute-start(bf16[3,64,128]{2,1,0:T(8,128)(2,1)S(1)} %slice.44), channel_id=1, source_target_pairs={{0,5},{1,4},{2,7},{3,6},{4,1},{5,0},{6,3},{7,2},{8,13},{9,12},{10,... | collective-permute-start | bytes 147464 | tf_op jit(solution)/shard_map/ppermute | solution.py:375
  12.4 1.8 %collective-permute-done.2 = bf16[3,64,128]{2,1,0:T(8,128)(2,1)S(1)} collective-permute-done((bf16[3,64,128]{2,1,0:T(8,128)(2,1)S(1)}, bf16[3,64,128]{2,1,0:T(8,128)(2,1)S(1)}, u32[]{:S(2)}, u32[]{:S(2)}) %collective-permute-start.2) | collective-permute-done | bytes 49184 | tf_op jit(solution)/shard_map/ppermute | solution.py:375
  14.2 2.0 %collective-permute-start.3 = (bf16[3,64,128]{2,1,0:T(8,128)(2,1)S(1)}, bf16[3,64,128]{2,1,0:T(8,128)(2,1)S(1)}, u32[]{:S(2)}, u32[]{:S(2)}) collective-permute-start(bf16[3,64,128]{2,1,0:T(8,128)(2,1)S(1)} %fusion.1), channel_id=1, source_target_pairs={{0,9},{1,8},{2,11},{3,10},{4,13},{5,12},{6,15},{7,14},{8,1},{9,0},... | collective-permute-start | bytes 147464 | tf_op jit(solution)/shard_map/ppermute | solution.py:375
  16.2 4.3 %collective-permute-start.5 = (bf16[64,128]{1,0:T(8,128)(2,1)S(1)}, bf16[64,128]{1,0:T(8,128)(2,1)S(1)}, u32[]{:S(2)}, u32[]{:S(2)}) collective-permute-start(bf16[64,128]{1,0:T(8,128)(2,1)S(1)} %get-tuple-element.34), channel_id=1, source_target_pairs={{0,31},{1,2},{2,1},{3,4},{4,3},{5,6},{6,5},{7,8},{8,7},{9,10},{10,... | collective-permute-start | bytes 49160 | tf_op jit(solution)/shard_map/ppermute | solution.py:375
  20.6 3.0 %local_levels.1 = (bf16[64,128,128]{2,1,0:T(8,128)(2,1)S(1)}, bf16[512,512]{1,0:T(8,128)(2,1)S(1)}, bf16[4,128,512]{2,1,0:T(8,128)(2,1)S(1)}) custom-call(bf16[4096,128]{1,0:T(8,128)(2,1)S(1)} %get-tuple-element.25.g_mid, f32[2560,128]{1,0:T(8,128)S(1)} %get-tuple-element.26.g_thin, bf16[8,4,128,128]{3,2,1,0:T(8,128)(2,1)S(1)} %get-tuple-element.27.restrict, ...), custom_call_target="tpu_custom_call" | custom-call | tf_op jit(solution)/shard_map/local_levels/pallas_call | solution.py:380
  23.6 2.3 %local_part.4.refs_0_ = f32[64,256,128]{2,1,0:T(8,128)S(1)} custom-call(bf16[64,256,128]{2,1,0:T(8,128)(2,1)S(1)} %get-tuple-element.21.fine_v, bf16[256,256]{1,0:T(8,128)(2,1)S(1)} %get-tuple-element.22.m1, bf16[256,256]{1,0:T(8,128)(2,1)S(1)} %get-tuple-element.23.mt1, bf16[256,128]{1,0:T(8,128)(2,1)S(1)} %get-tuple-element.24.mt2, ...), custom_call_target="tpu_custom_call" | custom-call | tf_op jit(solution)/shard_map/local_part/pallas_call | solution.py:399
  25.9 2.3 %local_part.5.refs_0_ = f32[64,256,128]{2,1,0:T(8,128)S(1)} custom-call(bf16[64,256,128]{2,1,0:T(8,128)(2,1)S(1)} %get-tuple-element.21.fine_v, bf16[256,256]{1,0:T(8,128)(2,1)S(1)} %get-tuple-element.22.m1, bf16[256,256]{1,0:T(8,128)(2,1)S(1)} %get-tuple-element.23.mt1, bf16[256,128]{1,0:T(8,128)(2,1)S(1)} %get-tuple-element.24.mt2, ...), custom_call_target="tpu_custom_call", output_to_operand_aliasing={{}: (7, {})} | custom-call | tf_op jit(solution)/shard_map/local_part/pallas_call | solution.py:399
  28.2 2.3 %local_part.6.refs_0_ = f32[64,256,128]{2,1,0:T(8,128)S(1)} custom-call(bf16[64,256,128]{2,1,0:T(8,128)(2,1)S(1)} %get-tuple-element.21.fine_v, bf16[256,256]{1,0:T(8,128)(2,1)S(1)} %get-tuple-element.22.m1, bf16[256,256]{1,0:T(8,128)(2,1)S(1)} %get-tuple-element.23.mt1, bf16[256,128]{1,0:T(8,128)(2,1)S(1)} %get-tuple-element.24.mt2, ...), custom_call_target="tpu_custom_call", output_to_operand_aliasing={{}: (7, {})} | custom-call | tf_op jit(solution)/shard_map/local_part/pallas_call | solution.py:399
  30.4 2.3 %local_part.7.res = f32[64,256,128]{2,1,0:T(8,128)S(1)} custom-call(bf16[64,256,128]{2,1,0:T(8,128)(2,1)S(1)} %get-tuple-element.21.fine_v, bf16[256,256]{1,0:T(8,128)(2,1)S(1)} %get-tuple-element.22.m1, bf16[256,256]{1,0:T(8,128)(2,1)S(1)} %get-tuple-element.23.mt1, bf16[256,128]{1,0:T(8,128)(2,1)S(1)} %get-tuple-element.24.mt2, ...), custom_call_target="tpu_custom_call", output_to_operand_aliasing={{}: (7, {})} | custom-call | tf_op jit(solution)/shard_map/local_part/pallas_call | solution.py:399
  32.7 0.0 collective-permute-done.3
  32.8 0.1 collective-permute-start.4
  32.9 4.2 %collective-permute-done.4 = bf16[2,64,128]{2,1,0:T(8,128)(2,1)S(1)} collective-permute-done((bf16[2,64,128]{2,1,0:T(8,128)(2,1)S(1)}, bf16[2,64,128]{2,1,0:T(8,128)(2,1)S(1)}, u32[]{:S(2)}, u32[]{:S(2)}) %collective-permute-start.4) | collective-permute-done | bytes 32800 | tf_op jit(solution)/shard_map/ppermute | solution.py:375
  37.1 0.0 collective-permute-done.5.halo_o
  37.1 4.3 %finish.1 = f32[64,256,128]{2,1,0:T(8,128)} custom-call(f32[64,256,128]{2,1,0:T(8,128)S(1)} %local_part.7.res, f32[4,64,128]{2,1,0:T(8,128)S(1)} %pad_maximum_fusion.sums, bf16[64,128]{1,0:T(8,128)(2,1)S(1)} %slice_bitcast_fusion.halo_r, bf16[64,128]{1,0:T(8,128)(2,1)S(1)} %collective-permute-done.5.halo_o, bf16[256,128]{1,0:T(8,128)(2,1)S(1)} %get-tuple-element.35.mtop, ...), custom_call_target="tpu_custom_call" | custom-call | tf_op jit(solution)/shard_map/finish/pallas_call | solution.py:435
  (11 shorter events, 0.1 us)
Async XLA Ops:
  4.1 1.5 %collective-permute-start = (bf16[5,64,128]{2,1,0:T(8,128)(2,1)S(1)}, bf16[5,64,128]{2,1,0:T(8,128)(2,1)S(1)}, u32[]{:S(2)}, u32[]{:S(2)}) collective-permute-start(bf16[5,64,128]{2,1,0:T(8,128)(2,1)S(1)} %get-tuple-element.33), channel_id=1, source_target_pairs={{0,1},{1,0},{2,3},{3,2},{4,5},{5,4},{6,7},{7,6},{8,9},{9,8},{10,11... | collective-permute-start | bytes 245768 | tf_op jit(solution)/shard_map/ppermute | solution.py:375
  5.6 4.8 %collective-permute-start.1 = (bf16[4,64,128]{2,1,0:T(8,128)(2,1)S(1)}, bf16[4,64,128]{2,1,0:T(8,128)(2,1)S(1)}, u32[]{:S(2)}, u32[]{:S(2)}) collective-permute-start(bf16[4,64,128]{2,1,0:T(8,128)(2,1)S(1)} %fusion), channel_id=1, source_target_pairs={{0,3},{1,2},{2,1},{3,0},{4,7},{5,6},{6,5},{7,4},{8,11},{9,10},{10,... | collective-permute-start | bytes 196616 | tf_op jit(solution)/shard_map/ppermute | solution.py:375
  10.4 3.8 %collective-permute-start.2 = (bf16[3,64,128]{2,1,0:T(8,128)(2,1)S(1)}, bf16[3,64,128]{2,1,0:T(8,128)(2,1)S(1)}, u32[]{:S(2)}, u32[]{:S(2)}) collective-permute-start(bf16[3,64,128]{2,1,0:T(8,128)(2,1)S(1)} %slice.44), channel_id=1, source_target_pairs={{0,5},{1,4},{2,7},{3,6},{4,1},{5,0},{6,3},{7,2},{8,13},{9,12},{10,... | collective-permute-start | bytes 147464 | tf_op jit(solution)/shard_map/ppermute | solution.py:375
  14.2 18.5 %collective-permute-start.3 = (bf16[3,64,128]{2,1,0:T(8,128)(2,1)S(1)}, bf16[3,64,128]{2,1,0:T(8,128)(2,1)S(1)}, u32[]{:S(2)}, u32[]{:S(2)}) collective-permute-start(bf16[3,64,128]{2,1,0:T(8,128)(2,1)S(1)} %fusion.1), channel_id=1, source_target_pairs={{0,9},{1,8},{2,11},{3,10},{4,13},{5,12},{6,15},{7,14},{8,1},{9,0},... | collective-permute-start | bytes 147464 | tf_op jit(solution)/shard_map/ppermute | solution.py:375
  16.2 20.9 %collective-permute-start.5 = (bf16[64,128]{1,0:T(8,128)(2,1)S(1)}, bf16[64,128]{1,0:T(8,128)(2,1)S(1)}, u32[]{:S(2)}, u32[]{:S(2)}) collective-permute-start(bf16[64,128]{1,0:T(8,128)(2,1)S(1)} %get-tuple-element.34), channel_id=1, source_target_pairs={{0,31},{1,2},{2,1},{3,4},{4,3},{5,6},{6,5},{7,8},{8,7},{9,10},{10,... | collective-permute-start | bytes 49160 | tf_op jit(solution)/shard_map/ppermute | solution.py:375
  32.8 4.3 %collective-permute-start.4 = (bf16[2,64,128]{2,1,0:T(8,128)(2,1)S(1)}, bf16[2,64,128]{2,1,0:T(8,128)(2,1)S(1)}, u32[]{:S(2)}, u32[]{:S(2)}) collective-permute-start(bf16[2,64,128]{2,1,0:T(8,128)(2,1)S(1)} %slice.45), channel_id=1, source_target_pairs={{0,17},{1,16},{2,19},{3,18},{4,21},{5,20},{6,23},{7,22},{8,25},{9,... | collective-permute-start | bytes 98312 | tf_op jit(solution)/shard_map/ppermute | solution.py:375
